TPU v7x, 32 devices: a whole 2x2x4 slice. The times are simulated.
32 devices in a mesh: tm: 2 (over x), member: 4 (over y, core), state: 4 (over z).
Axes of the slice: x: 2, y: 2, z: 4, core: 2. Of those that a mesh axis runs over, the one named last changes fastest.
Arguments:
- members: bfloat16 [4, 8, 16, 192, 1536], P('tm', 'member', None, 'state'), may hold values from -6 to 6
- slot_grad: float32 [4, 16, 192, 1536], P('tm', None, 'state'), may hold values from -6 to 6
- diffusivity: float32 [192, 1536], P('state'), may hold values from 0.03 to 0.24
- vertical: float32 [16, 16], replicated, may hold values from -0.3 to 2.1, as said below
Outputs:
- control_gradient: float32 [16, 8, 192, 1536], P('tm', 'member', 'state')
Inputs may be any that keep to these rules, and one draw needn't show every extreme that they name: `vertical`: the diagonal entries lie between 0.5 and 2.1.
All inputs are finite; a program needn't handle non-finite values.
Results may differ from a plain program's by a relative error of at most 0.0003.
Values sent between devices are 32-bit elements; how exact they have to be, the bound alone decides.
No kernel may reach another device: no remote copies, remote signals or barrier semaphores. Data moves between devices by JAX's collectives and lax.ppermute only.
A program may use at most 128 MiB of HBM per device.

v0:
```python
import functools

import jax
import jax.numpy as jnp
from jax import lax
from jax.experimental import pallas as pl
from jax.experimental.pallas import tpu as pltpu
from jax.sharding import PartitionSpec as P


NSTEP = 4
SUB = 8


def level_chunks(count):
    sizes, left = [], count
    while left > 0:
        size = max(left // 2, 1)
        sizes.append(size)
        left -= size
    starts = [sum(sizes[:i]) for i in range(len(sizes))]
    return list(zip(starts, sizes))


def divisor(length, unit, most):
    best = unit
    for size in range(unit, most + 1, unit):
        if length % size == 0:
            best = size
    return best


def mix_kernel(chunks, lanes, w_ref, members_ref, grad_ref, *out_refs):
    slots, ensemble, levels, rows, cols = members_ref.shape
    w = w_ref[...]
    high = w.astype(jnp.bfloat16)
    low = (w - high.astype(jnp.float32)).astype(jnp.bfloat16)
    twice = jnp.concatenate([high, high], axis=1)

    def piece(index, carry):
        at = pl.ds(pl.multiple_of(index * lanes, lanes), lanes)
        grads = [grad_ref[s, :, :, at] for s in range(slots)]
        for k in range(ensemble):
            product = members_ref[0, k, :, :, at].astype(jnp.float32) * grads[0]
            for s in range(1, slots):
                product += members_ref[s, k, :, :, at].astype(jnp.float32) * grads[s]
            for first in range(0, rows, SUB):
                x = product[:, first : first + SUB].reshape(levels * SUB, lanes)
                x_high = x.astype(jnp.bfloat16)
                x_low = (x - x_high.astype(jnp.float32)).astype(jnp.bfloat16)
                y = jnp.dot(
                    twice,
                    jnp.concatenate([x_high, x_low], axis=0),
                    preferred_element_type=jnp.float32,
                ) + jnp.dot(low, x_high, preferred_element_type=jnp.float32)
                y = y.reshape(-1, SUB, lanes)
                for out_ref, (start, size) in zip(out_refs, chunks):
                    out_ref[:, k, first : first + SUB, at] = y[start : start + size]
        return carry

    lax.fori_loop(0, cols // lanes, piece, 0)


def mixed_levels(members, slot_grad, weights, chunks):
    slots, ensemble, levels, rows, cols = members.shape
    row_block, col_block = divisor(rows, SUB, 16), divisor(cols, 128, 512)
    lanes = divisor(col_block, 128, 256)
    shapes = [(size, ensemble, rows, cols) for _, size in chunks]
    own = weights.shape[0] // SUB
    return pl.pallas_call(
        functools.partial(mix_kernel, chunks, lanes),
        grid=(rows // row_block, cols // col_block),
        in_specs=[
            pl.BlockSpec(weights.shape, lambda i, j: (0, 0)),
            pl.BlockSpec(
                (slots, ensemble, levels, row_block, col_block), lambda i, j: (0, 0, 0, i, j)
            ),
            pl.BlockSpec((slots, levels, row_block, col_block), lambda i, j: (0, 0, i, j)),
        ],
        out_specs=[
            pl.BlockSpec((size, ensemble, row_block, col_block), lambda i, j: (0, 0, i, j))
            for _, size in chunks
        ],
        out_shape=[jax.ShapeDtypeStruct(shape, jnp.float32) for shape in shapes],
        cost_estimate=pl.CostEstimate(
            flops=6 * SUB * levels * own * ensemble * rows * cols,
            bytes_accessed=2 * members.size + 4 * slot_grad.size,
            transcendentals=0,
        ),
        name="mix",
    )(weights, members, slot_grad)


def filter_kernel(parts, halo, share, *refs):
    field_refs = refs[:parts]
    sum_ref, other_ref, above_ref, below_ref, rate_ref = refs[parts : parts + 5]
    out_ref, f_ref, v_ref = refs[-3:]
    rows, cols = out_ref.shape[2:]
    bands = rows // SUB + 2
    blank = jnp.zeros((SUB, cols), jnp.float32)
    for edge in (0, bands + 1):
        v_ref[edge * SUB : (edge + 1) * SUB] = blank
    for edge in (0, bands - 1):
        f_ref[edge * SUB : (edge + 1) * SUB] = blank
    f_ref[SUB - halo : SUB] = above_ref[0, 0]
    f_ref[SUB + rows : SUB + rows + halo] = below_ref[0, 0]
    for band in range(rows // SUB):
        at = slice(band * SUB, (band + 1) * SUB)
        value = field_refs[0][0, 0, at]
        for ref in field_refs[1:]:
            value += ref[0, 0, at]
        f_ref[SUB + band * SUB : SUB + (band + 1) * SUB] = value - share * (
            sum_ref[0, at] + other_ref[0, at]
        )
    for step in range(NSTEP):
        for band in range(bands):
            at = slice(band * SUB, (band + 1) * SUB)
            v_ref[SUB + band * SUB : 2 * SUB + band * SUB] = rate_ref[at] * f_ref[at]
        last = step == NSTEP - 1
        for band in range(1, bands - 1) if last else range(bands):
            at = slice(band * SUB, (band + 1) * SUB)
            base = SUB + band * SUB
            v = v_ref[base : base + SUB]
            value = (
                f_ref[at]
                + v_ref[base + 1 : base + 1 + SUB]
                + v_ref[base - 1 : base - 1 + SUB]
                + pltpu.roll(v, 1, 1)
                + pltpu.roll(v, cols - 1, 1)
                - 4.0 * v
            )
            if last:
                out_ref[0, 0, (band - 1) * SUB : band * SUB] = value
            else:
                f_ref[at] = value


def filtered(fields, sums, halos, rate, start, total, ensemble, previous):
    size, members, rows, cols = fields[0].shape
    halo = halos[0].shape[2]
    plane = pl.BlockSpec((1, 1, rows, cols), lambda i, k: (i, k, 0, 0))
    shared = pl.BlockSpec((1, rows, cols), lambda i, k: (i, 0, 0))
    edge = pl.BlockSpec((1, 1, halo, cols), lambda i, k: (i, k, 0, 0))
    operands = [*fields, *sums, *halos, rate]
    in_specs = [plane] * len(fields) + [shared] * 2 + [edge] * 2
    in_specs.append(pl.BlockSpec(rate.shape, lambda i, k: (0, 0)))
    aliases = {}
    if previous is not None:
        aliases = {len(operands): 0}
        operands.append(previous)
        in_specs.append(pl.BlockSpec(memory_space=pl.ANY))
    return pl.pallas_call(
        functools.partial(filter_kernel, len(fields), halo, 1.0 / ensemble),
        grid=(size, members),
        in_specs=in_specs,
        out_specs=pl.BlockSpec((1, 1, rows, cols), lambda i, k: (i + start, k, 0, 0)),
        out_shape=jax.ShapeDtypeStruct((total, members, rows, cols), jnp.float32),
        scratch_shapes=[
            pltpu.VMEM((rows + 2 * SUB, cols), jnp.float32),
            pltpu.VMEM((rows + 4 * SUB, cols), jnp.float32),
        ],
        input_output_aliases=aliases,
        cost_estimate=pl.CostEstimate(
            flops=40 * NSTEP * size * members * rows * cols,
            bytes_accessed=16 * size * members * rows * cols,
            transcendentals=0,
        ),
        name="filter",
    )(*operands)


def edges_from_neighbours(top, bottom):
    size = lax.axis_size("state")
    up = [(i, i + 1) for i in range(size - 1)]
    down = [(j, i) for i, j in up]
    return lax.ppermute(bottom, "state", up), lax.ppermute(top, "state", down)


def halves_of_sum(value):
    size = lax.axis_size("member")
    reach = 1
    other = jnp.zeros_like(value)
    if size & (size - 1):
        value, other = lax.psum(value, "member"), other
        return value, other
    while reach < size:
        pairs = [(i, i ^ reach) for i in range(size)]
        value = value + other if reach > 1 else value
        other = lax.ppermute(value, "member", pairs)
        reach *= 2
    return value, other


def compute(members, slot_grad, diffusivity, vertical):
    ensemble = members.shape[1] * lax.axis_size("member")
    levels, rows = members.shape[2:4]
    groups = lax.axis_size("tm")
    own = levels // groups
    here = lax.axis_index("tm")
    chunks = level_chunks(own)
    halo = NSTEP
    scaled = vertical.T * float(ensemble - 1) ** (-0.5)
    eye = jnp.eye(SUB, dtype=jnp.float32)

    def weights(shift):
        first = lax.rem(here + shift, groups) * own
        chosen = lax.dynamic_slice_in_dim(scaled, first, own, 0)
        return (chosen[:, None, :, None] * eye[None, :, None, :]).reshape(own * SUB, levels * SUB)

    arrived = []
    for shift in range(1, groups):
        outgoing = mixed_levels(members, slot_grad, weights(shift), chunks)
        pairs = [(i, (i + shift) % groups) for i in range(groups)]
        parts = []
        for part in outgoing:
            parts.append(lax.ppermute(part, "tm", pairs))
        arrived.append(parts)
    mine = mixed_levels(members, slot_grad, weights(0), chunks)

    above, below = edges_from_neighbours(diffusivity[:halo], diffusivity[rows - halo :])
    blank = jnp.zeros((SUB - halo, diffusivity.shape[1]), jnp.float32)
    rate = jnp.concatenate([blank, above, diffusivity, below, blank], axis=0)

    staged, before = [], None
    for index in range(len(chunks)):
        received = [parts[index] for parts in arrived]
        if before is not None:
            received, before = lax.optimization_barrier((received, before))
        fields = [mine[index]] + received
        local = functools.reduce(jnp.add, [f[:, k] for f in fields for k in range(f.shape[1])])
        before, other = halves_of_sum(local)
        staged.append([fields, before, other])

    result = None
    for index, (start, size) in enumerate(chunks):
        fields, *sums = staged[index]
        if index + 1 < len(chunks):
            sums, _ = lax.optimization_barrier((sums, staged[index + 1][1]))

        def edge(at):
            value = functools.reduce(jnp.add, [f[:, :, at] for f in fields])
            return value - (sums[0][:, at] + sums[1][:, at])[:, None] * (1.0 / ensemble)

        halos = edges_from_neighbours(edge(slice(0, halo)), edge(slice(rows - halo, rows)))
        result = filtered(fields, sums, halos, rate, start, own, ensemble, result)
    return result


def solution(mesh):
    in_specs = (
        P("tm", "member", None, "state", None),
        P("tm", None, "state", None),
        P("state", None),
        P(),
    )
    out_specs = P("tm", "member", "state", None)
    return jax.shard_map(compute, mesh=mesh, in_specs=in_specs, out_specs=out_specs, check_vma=False)
```

profile of v0, /device:TPU:24, one launch (start us, length us, event | category | flops | bytes accessed | tf_op | source)
XLA Modules:
  0.0 211.7 jit_solution(4173546637348649984)
XLA Ops:
  1.9 13.3 %mix.3 = (f32[4,2,48,1536]{3,2,1,0:T(8,128)}, f32[2,2,48,1536]{3,2,1,0:T(8,128)}, f32[1,2,48,1536]{3,2,1,0:T(8,128)}, f32[1,2,48,1536]{3,2,1,0:T(8,128)}) custom-call(f32[64,128]{1,0:T(8,128)} %mul.117.w_ref, bf16[2,2,16,48,1536]{4,3,2,1,0:T(8,128)(2,1)} %members_ref.3, f32[2,16,48,1536]{3,2,1,0:T(8,128)} %grad_ref.3), custom_call_target="tpu_custom_call" | custom-call | flops 905969664 | bytes 18874368 | tf_op jit(solution)/shard_map/mix/pallas_call | solution.py:70
  15.2 1.5 collective-permute-start.3
  17.6 13.4 %mix.2 = (f32[4,2,48,1536]{3,2,1,0:T(8,128)}, f32[2,2,48,1536]{3,2,1,0:T(8,128)}, f32[1,2,48,1536]{3,2,1,0:T(8,128)}, f32[1,2,48,1536]{3,2,1,0:T(8,128)}) custom-call(f32[64,128]{1,0:T(8,128)} %mul.113.w_ref, bf16[2,2,16,48,1536]{4,3,2,1,0:T(8,128)(2,1)} %members_ref.3, f32[2,16,48,1536]{3,2,1,0:T(8,128)} %grad_ref.3), custom_call_target="tpu_custom_call" | custom-call | flops 905969664 | bytes 18874368 | tf_op jit(solution)/shard_map/mix/pallas_call | solution.py:70
  31.0 37.5 %collective-permute-done.3.refs_1_ = f32[4,2,48,1536]{3,2,1,0:T(8,128)S(1)} collective-permute-done((f32[4,2,48,1536]{3,2,1,0:T(8,128)}, f32[4,2,48,1536]{3,2,1,0:T(8,128)S(1)}, u32[]{:S(2)}, u32[]{:S(2)}) %collective-permute-start.3) | collective-permute-done | bytes 2359328 | tf_op jit(solution)/shard_map/ppermute | solution.py:216
  68.5 2.9 %fusion = f32[4,48,1536]{2,1,0:T(8,128)S(1)} fusion(f32[4,2,48,1536]{3,2,1,0:T(8,128)S(1)} %collective-permute-done.3.refs_1_, f32[4,2,48,1536]{3,2,1,0:T(8,128)} %get-tuple-element.28.refs_0_), kind=kLoop, calls=%fused_computation.1 | loop fusion | flops 884736 | bytes 5898240 | tf_op jit(solution)/shard_map/add | solution.py:230
  71.5 1.6 collective-permute-start.2
  74.4 25.4 %collective-permute-done.2.refs_1_ = f32[2,2,48,1536]{3,2,1,0:T(8,128)S(1)} collective-permute-done((f32[2,2,48,1536]{3,2,1,0:T(8,128)S(1)}, f32[2,2,48,1536]{3,2,1,0:T(8,128)S(1)}, u32[]{:S(2)}, u32[]{:S(2)}) %collective-permute-start.2) | collective-permute-done | bytes 1179680 | tf_op jit(solution)/shard_map/ppermute | solution.py:216
  101.3 1.5 collective-permute-start.1
  103.4 1.6 collective-permute-start.16
  105.0 12.5 %collective-permute-done.1.refs_1_ = f32[1,2,48,1536]{3,2,1,0:T(8,128)S(1)} collective-permute-done((f32[1,2,48,1536]{3,2,1,0:T(8,128)S(1)}, f32[1,2,48,1536]{3,2,1,0:T(8,128)S(1)}, u32[]{:S(2)}, u32[]{:S(2)}) %collective-permute-start.1) | collective-permute-done | bytes 589856 | tf_op jit(solution)/shard_map/ppermute | solution.py:216
  118.7 1.3 collective-permute-start.11
  120.0 4.5 %collective-permute-start.12 = (f32[4,1536]{1,0:T(4,128)S(1)}, f32[4,1536]{1,0:T(4,128)S(1)}, u32[]{:S(2)}, u32[]{:S(2)}) collective-permute-start(f32[4,1536]{1,0:T(4,128)S(1)} %get-tuple-element.55), channel_id=1, source_target_pairs={{1,0},{2,1},{3,2},{5,4},{6,5},{7,6},{9,8},{10,9},{11,10},{13,12},{... | collective-permute-start | bytes 73736 | tf_op jit(solution)/shard_map/ppermute | solution.py:176
  124.6 1.6 collective-permute-start.19
  126.2 2.5 %collective-permute-done.refs_1_ = f32[1,2,48,1536]{3,2,1,0:T(8,128)S(1)} collective-permute-done((f32[1,2,48,1536]{3,2,1,0:T(8,128)S(1)}, f32[1,2,48,1536]{3,2,1,0:T(8,128)S(1)}, u32[]{:S(2)}, u32[]{:S(2)}) %collective-permute-start) | collective-permute-done | bytes 589856 | tf_op jit(solution)/shard_map/ppermute | solution.py:216
  128.7 1.5 collective-permute-start.13
  131.2 22.3 %collective-permute-done.19.refs_3_ = f32[4,48,1536]{2,1,0:T(8,128)S(1)} collective-permute-done((f32[4,48,1536]{2,1,0:T(8,128)S(1)}, f32[4,48,1536]{2,1,0:T(8,128)S(1)}, u32[]{:S(2)}, u32[]{:S(2)}) %collective-permute-start.19) | collective-permute-done | bytes 1179680 | tf_op jit(solution)/shard_map/ppermute | solution.py:189
  153.5 1.3 collective-permute-start.17
  154.8 5.2 %collective-permute-start.18 = (f32[2,2,4,1536]{3,2,1,0:T(4,128)}, f32[2,2,4,1536]{3,2,1,0:T(4,128)}, u32[]{:S(2)}, u32[]{:S(2)}) collective-permute-start(f32[2,2,4,1536]{3,2,1,0:T(4,128)} %get-tuple-element.43), channel_id=1, source_target_pairs={{1,0},{2,1},{3,2},{5,4},{6,5},{7,6},{9,8},{10,9},{11,10},{13,12},{... | collective-permute-start | bytes 294920 | tf_op jit(solution)/shard_map/ppermute | solution.py:176
  160.1 1.6 collective-permute-start.8
  161.8 1.3 fusion.1
  163.2 3.7 %collective-permute-done.8.refs_3_ = f32[1,48,1536]{2,1,0:T(8,128)S(1)} collective-permute-done((f32[1,48,1536]{2,1,0:T(8,128)S(1)}, f32[1,48,1536]{2,1,0:T(8,128)S(1)}, u32[]{:S(2)}, u32[]{:S(2)}) %collective-permute-start.8) | collective-permute-done | bytes 294944 | tf_op jit(solution)/shard_map/ppermute | solution.py:189
  166.9 1.3 collective-permute-start.20
  168.2 4.6 %collective-permute-start.21 = (f32[4,2,4,1536]{3,2,1,0:T(4,128)S(1)}, f32[4,2,4,1536]{3,2,1,0:T(4,128)S(1)}, u32[]{:S(2)}, u32[]{:S(2)}) collective-permute-start(f32[4,2,4,1536]{3,2,1,0:T(4,128)S(1)} %get-tuple-element.39), channel_id=1, source_target_pairs={{1,0},{2,1},{3,2},{5,4},{6,5},{7,6},{9,8},{10,9},{11,10},{13,12},{... | collective-permute-start | bytes 589832 | tf_op jit(solution)/shard_map/ppermute | solution.py:176
  172.8 1.3 collective-permute-start.14
  174.1 4.5 %collective-permute-start.15 = (f32[1,2,4,1536]{3,2,1,0:T(4,128)S(1)}, f32[1,2,4,1536]{3,2,1,0:T(4,128)S(1)}, u32[]{:S(2)}, u32[]{:S(2)}) collective-permute-start(f32[1,2,4,1536]{3,2,1,0:T(4,128)S(1)} %get-tuple-element.47), channel_id=1, source_target_pairs={{1,0},{2,1},{3,2},{5,4},{6,5},{7,6},{9,8},{10,9},{11,10},{13,12},{... | collective-permute-start | bytes 147464 | tf_op jit(solution)/shard_map/ppermute | solution.py:176
  178.7 1.9 collective-permute-start.10
  180.7 1.3 collective-permute-start.9
  182.0 2.0 concatenate.3.refs_6_
  184.1 10.8 %filter.4.refs_7_ = f32[8,2,48,1536]{3,2,1,0:T(8,128)} custom-call(f32[4,2,48,1536]{3,2,1,0:T(8,128)} %get-tuple-element.28.refs_0_, f32[4,2,48,1536]{3,2,1,0:T(8,128)} %copy-done, f32[4,48,1536]{2,1,0:T(8,128)} %copy-done.1, f32[4,48,1536]{2,1,0:T(8,128)} %copy-done.9, f32[4,2,4,1536]{3,2,1,0:T(4,128)} %copy-done.16, f32[4,2,4,1536]{3,2,1,0:T(4,128)} %copy-done.17, ...), custom_call_target="tpu_custom_call" | custom-call | flops 94371840 | bytes 9437184 | tf_op jit(solution)/shard_map/filter/pallas_call | solution.py:152
  194.9 6.4 %filter.5.refs_7_ = f32[8,2,48,1536]{3,2,1,0:T(8,128)} custom-call(f32[2,2,48,1536]{3,2,1,0:T(8,128)} %get-tuple-element.26.refs_0_, f32[2,2,48,1536]{3,2,1,0:T(8,128)} %copy-done.3, f32[2,48,1536]{2,1,0:T(8,128)} %copy-done.4, f32[2,48,1536]{2,1,0:T(8,128)} %copy-done.12, f32[2,2,4,1536]{3,2,1,0:T(4,128)} %copy-done.18, ...), custom_call_target="tpu_custom_call", output_to_operand_aliasing={{}: (7, {})} | custom-call | flops 47185920 | bytes 4718592 | tf_op jit(solution)/shard_map/filter/pallas_call | solution.py:152
  202.5 4.0 %filter.6.refs_7_ = f32[8,2,48,1536]{3,2,1,0:T(8,128)} custom-call(f32[1,2,48,1536]{3,2,1,0:T(8,128)} %get-tuple-element.24.refs_0_, f32[1,2,48,1536]{3,2,1,0:T(8,128)} %copy-done.8, f32[1,48,1536]{2,1,0:T(8,128)} %copy-done.10, f32[1,48,1536]{2,1,0:T(8,128)} %copy-done.13, f32[1,2,4,1536]{3,2,1,0:T(4,128)} %copy-done.19, ...), custom_call_target="tpu_custom_call", output_to_operand_aliasing={{}: (7, {})} | custom-call | flops 23592960 | bytes 2359296 | tf_op jit(solution)/shard_map/filter/pallas_call | solution.py:152
  207.7 4.0 %filter.7 = f32[8,2,48,1536]{3,2,1,0:T(8,128)} custom-call(f32[1,2,48,1536]{3,2,1,0:T(8,128)} %get-tuple-element.22.refs_0_, f32[1,2,48,1536]{3,2,1,0:T(8,128)} %copy-done.7, f32[1,48,1536]{2,1,0:T(8,128)} %copy-done.11, f32[1,48,1536]{2,1,0:T(8,128)} %copy-done.14, f32[1,2,4,1536]{3,2,1,0:T(4,128)} %copy-done.22, ...), custom_call_target="tpu_custom_call", output_to_operand_aliasing={{}: (7, {})} | custom-call | flops 23592960 | bytes 2359296 | tf_op jit(solution)/shard_map/filter/pallas_call | solution.py:152
  (97 shorter events, 11.2 us)
Async XLA Ops:
  15.2 53.2 %collective-permute-start.3 = (f32[4,2,48,1536]{3,2,1,0:T(8,128)}, f32[4,2,48,1536]{3,2,1,0:T(8,128)S(1)}, u32[]{:S(2)}, u32[]{:S(2)}) collective-permute-start(f32[4,2,48,1536]{3,2,1,0:T(8,128)} %get-tuple-element.29), channel_id=1, source_target_pairs={{0,16},{16,0},{1,17},{17,1},{2,18},{18,2},{3,19},{19,3},{4,20},{20... | collective-permute-start | bytes 7077896 | tf_op jit(solution)/shard_map/ppermute | solution.py:216
  68.5 93.4 %copy-start = (f32[4,2,48,1536]{3,2,1,0:T(8,128)}, f32[4,2,48,1536]{3,2,1,0:T(8,128)S(1)}, u32[]{:S(2)}) copy-start(f32[4,2,48,1536]{3,2,1,0:T(8,128)S(1)} %collective-permute-done.3.refs_1_) | copy-start | bytes 7077892
  71.4 2.9 %collective-permute-start.4 = (f32[4,48,1536]{2,1,0:T(8,128)S(1)}, f32[4,48,1536]{2,1,0:T(8,128)S(1)}, u32[]{:S(2)}, u32[]{:S(2)}) collective-permute-start(f32[4,48,1536]{2,1,0:T(8,128)S(1)} %fusion), channel_id=1, source_target_pairs={{0,4},{4,0},{8,12},{12,8},{1,5},{5,1},{9,13},{13,9},{2,6},{6,2},{1... | collective-permute-start | bytes 3538952 | tf_op jit(solution)/shard_map/ppermute | solution.py:189
  71.5 28.4 %copy-start.2 = (f32[2,2,48,1536]{3,2,1,0:T(8,128)S(1)}, f32[2,2,48,1536]{3,2,1,0:T(8,128)}, u32[]{:S(2)}) copy-start(f32[2,2,48,1536]{3,2,1,0:T(8,128)} %get-tuple-element.26.refs_0_) | copy-start | bytes 3538948
  71.5 28.4 %collective-permute-start.2 = (f32[2,2,48,1536]{3,2,1,0:T(8,128)S(1)}, f32[2,2,48,1536]{3,2,1,0:T(8,128)S(1)}, u32[]{:S(2)}, u32[]{:S(2)}) collective-permute-start(f32[2,2,48,1536]{3,2,1,0:T(8,128)S(1)} %copy-done.23), channel_id=1, source_target_pairs={{0,16},{16,0},{1,17},{17,1},{2,18},{18,2},{3,19},{19,3},{4,20},{20... | collective-permute-start | bytes 3538952 | tf_op jit(solution)/shard_map/ppermute | solution.py:216
  74.4 87.2 %copy-start.1 = (f32[4,48,1536]{2,1,0:T(8,128)}, f32[4,48,1536]{2,1,0:T(8,128)S(1)}, u32[]{:S(2)}) copy-start(f32[4,48,1536]{2,1,0:T(8,128)S(1)} %add.182.refs_2_) | copy-start | bytes 3538948
  99.8 30.7 %copy-start.3 = (f32[2,2,48,1536]{3,2,1,0:T(8,128)}, f32[2,2,48,1536]{3,2,1,0:T(8,128)S(1)}, u32[]{:S(2)}) copy-start(f32[2,2,48,1536]{3,2,1,0:T(8,128)S(1)} %collective-permute-done.2.refs_1_) | copy-start | bytes 3538948
  100.0 3.4 %collective-permute-start.5 = (f32[2,48,1536]{2,1,0:T(8,128)S(1)}, f32[2,48,1536]{2,1,0:T(8,128)S(1)}, u32[]{:S(2)}, u32[]{:S(2)}) collective-permute-start(f32[2,48,1536]{2,1,0:T(8,128)S(1)} %add_bitcast_fusion), channel_id=1, source_target_pairs={{0,4},{4,0},{8,12},{12,8},{1,5},{5,1},{9,13},{13,9},{2,6},{6,2},{1... | collective-permute-start | bytes 1769480 | tf_op jit(solution)/shard_map/ppermute | solution.py:189
  101.3 16.2 %collective-permute-start.1 = (f32[1,2,48,1536]{3,2,1,0:T(8,128)S(1)}, f32[1,2,48,1536]{3,2,1,0:T(8,128)S(1)}, u32[]{:S(2)}, u32[]{:S(2)}) collective-permute-start(f32[1,2,48,1536]{3,2,1,0:T(8,128)S(1)} %copy-done.25), channel_id=1, source_target_pairs={{0,16},{16,0},{1,17},{17,1},{2,18},{18,2},{3,19},{19,3},{4,20},{20... | collective-permute-start | bytes 1769480 | tf_op jit(solution)/shard_map/ppermute | solution.py:216
  102.8 25.9 %collective-permute-start = (f32[1,2,48,1536]{3,2,1,0:T(8,128)S(1)}, f32[1,2,48,1536]{3,2,1,0:T(8,128)S(1)}, u32[]{:S(2)}, u32[]{:S(2)}) collective-permute-start(f32[1,2,48,1536]{3,2,1,0:T(8,128)S(1)} %copy-done.24), channel_id=1, source_target_pairs={{0,16},{16,0},{1,17},{17,1},{2,18},{18,2},{3,19},{19,3},{4,20},{20... | collective-permute-start | bytes 1769480 | tf_op jit(solution)/shard_map/ppermute | solution.py:216
  103.4 27.0 %copy-start.4 = (f32[2,48,1536]{2,1,0:T(8,128)}, f32[2,48,1536]{2,1,0:T(8,128)S(1)}, u32[]{:S(2)}) copy-start(f32[2,48,1536]{2,1,0:T(8,128)S(1)} %add.186.refs_2_) | copy-start | bytes 1769476
  103.4 26.9 %collective-permute-start.16 = (f32[2,48,1536]{2,1,0:T(8,128)S(1)}, f32[2,48,1536]{2,1,0:T(8,128)S(1)}, u32[]{:S(2)}, u32[]{:S(2)}) collective-permute-start(f32[2,48,1536]{2,1,0:T(8,128)S(1)} %add.186.refs_2_), channel_id=1, source_target_pairs={{0,8},{4,12},{8,0},{12,4},{1,9},{5,13},{9,1},{13,5},{2,10},{6,14},... | collective-permute-start | bytes 1769480 | tf_op jit(solution)/shard_map/ppermute | solution.py:189
  117.5 45.6 %copy-start.8 = (f32[1,2,48,1536]{3,2,1,0:T(8,128)}, f32[1,2,48,1536]{3,2,1,0:T(8,128)S(1)}, u32[]{:S(2)}) copy-start(f32[1,2,48,1536]{3,2,1,0:T(8,128)S(1)} %collective-permute-done.1.refs_1_) | copy-start | bytes 1769476
  117.6 7.0 %collective-permute-start.6 = (f32[1,48,1536]{2,1,0:T(8,128)S(1)}, f32[1,48,1536]{2,1,0:T(8,128)S(1)}, u32[]{:S(2)}, u32[]{:S(2)}) collective-permute-start(f32[1,48,1536]{2,1,0:T(8,128)S(1)} %add_bitcast_fusion.2), channel_id=1, source_target_pairs={{0,4},{4,0},{8,12},{12,8},{1,5},{5,1},{9,13},{13,9},{2,6},{6,2},{1... | collective-permute-start | bytes 884744 | tf_op jit(solution)/shard_map/ppermute | solution.py:189
  118.7 49.4 %collective-permute-start.11 = (f32[4,1536]{1,0:T(4,128)S(1)}, f32[4,1536]{1,0:T(4,128)S(1)}, u32[]{:S(2)}, u32[]{:S(2)}) collective-permute-start(f32[4,1536]{1,0:T(4,128)S(1)} %get-tuple-element.56), channel_id=1, source_target_pairs={{0,1},{1,2},{2,3},{4,5},{5,6},{6,7},{8,9},{9,10},{10,11},{12,13},{... | collective-permute-start | bytes 73736 | tf_op jit(solution)/shard_map/ppermute | solution.py:176
  120.0 52.7 %collective-permute-start.12 = (f32[4,1536]{1,0:T(4,128)S(1)}, f32[4,1536]{1,0:T(4,128)S(1)}, u32[]{:S(2)}, u32[]{:S(2)}) collective-permute-start(f32[4,1536]{1,0:T(4,128)S(1)} %get-tuple-element.55), channel_id=1, source_target_pairs={{1,0},{2,1},{3,2},{5,4},{6,5},{7,6},{9,8},{10,9},{11,10},{13,12},{... | collective-permute-start | bytes 73736 | tf_op jit(solution)/shard_map/ppermute | solution.py:176
  124.6 28.9 %collective-permute-start.19 = (f32[4,48,1536]{2,1,0:T(8,128)S(1)}, f32[4,48,1536]{2,1,0:T(8,128)S(1)}, u32[]{:S(2)}, u32[]{:S(2)}) collective-permute-start(f32[4,48,1536]{2,1,0:T(8,128)S(1)} %add.182.refs_2_), channel_id=1, source_target_pairs={{0,8},{4,12},{8,0},{12,4},{1,9},{5,13},{9,1},{13,5},{2,10},{6,14},... | collective-permute-start | bytes 3538952 | tf_op jit(solution)/shard_map/ppermute | solution.py:189
  126.2 35.5 %copy-start.10 = (f32[1,48,1536]{2,1,0:T(8,128)}, f32[1,48,1536]{2,1,0:T(8,128)S(1)}, u32[]{:S(2)}) copy-start(f32[1,48,1536]{2,1,0:T(8,128)S(1)} %add.190.refs_2_) | copy-start | bytes 884740
  128.7 49.9 %copy-start.7 = (f32[1,2,48,1536]{3,2,1,0:T(8,128)}, f32[1,2,48,1536]{3,2,1,0:T(8,128)S(1)}, u32[]{:S(2)}) copy-start(f32[1,2,48,1536]{3,2,1,0:T(8,128)S(1)} %collective-permute-done.refs_1_) | copy-start | bytes 1769476
  128.7 31.3 %collective-permute-start.13 = (f32[1,48,1536]{2,1,0:T(8,128)S(1)}, f32[1,48,1536]{2,1,0:T(8,128)S(1)}, u32[]{:S(2)}, u32[]{:S(2)}) collective-permute-start(f32[1,48,1536]{2,1,0:T(8,128)S(1)} %add.190.refs_2_), channel_id=1, source_target_pairs={{0,8},{4,12},{8,0},{12,4},{1,9},{5,13},{9,1},{13,5},{2,10},{6,14},... | collective-permute-start | bytes 884744 | tf_op jit(solution)/shard_map/ppermute | solution.py:189
  130.3 31.4 %copy-start.12 = (f32[2,48,1536]{2,1,0:T(8,128)}, f32[2,48,1536]{2,1,0:T(8,128)S(1)}, u32[]{:S(2)}) copy-start(f32[2,48,1536]{2,1,0:T(8,128)S(1)} %collective-permute-done.16.refs_3_) | copy-start | bytes 1769476
  130.4 24.4 %collective-permute-start.7 = (f32[1,48,1536]{2,1,0:T(8,128)S(1)}, f32[1,48,1536]{2,1,0:T(8,128)S(1)}, u32[]{:S(2)}, u32[]{:S(2)}) collective-permute-start(f32[1,48,1536]{2,1,0:T(8,128)S(1)} %add_bitcast_fusion.1), channel_id=1, source_target_pairs={{0,4},{4,0},{8,12},{12,8},{1,5},{5,1},{9,13},{13,9},{2,6},{6,2},{1... | collective-permute-start | bytes 884744 | tf_op jit(solution)/shard_map/ppermute | solution.py:189
  153.5 20.6 %collective-permute-start.17 = (f32[2,2,4,1536]{3,2,1,0:T(4,128)S(1)}, f32[2,2,4,1536]{3,2,1,0:T(4,128)S(1)}, u32[]{:S(2)}, u32[]{:S(2)}) collective-permute-start(f32[2,2,4,1536]{3,2,1,0:T(4,128)S(1)} %get-tuple-element.44), channel_id=1, source_target_pairs={{0,1},{1,2},{2,3},{4,5},{5,6},{6,7},{8,9},{9,10},{10,11},{12,13},{... | collective-permute-start | bytes 294920 | tf_op jit(solution)/shard_map/ppermute | solution.py:176
  154.8 40.1 %collective-permute-start.18 = (f32[2,2,4,1536]{3,2,1,0:T(4,128)}, f32[2,2,4,1536]{3,2,1,0:T(4,128)}, u32[]{:S(2)}, u32[]{:S(2)}) collective-permute-start(f32[2,2,4,1536]{3,2,1,0:T(4,128)} %get-tuple-element.43), channel_id=1, source_target_pairs={{1,0},{2,1},{3,2},{5,4},{6,5},{7,6},{9,8},{10,9},{11,10},{13,12},{... | collective-permute-start | bytes 294920 | tf_op jit(solution)/shard_map/ppermute | solution.py:176
  160.1 6.8 %collective-permute-start.8 = (f32[1,48,1536]{2,1,0:T(8,128)S(1)}, f32[1,48,1536]{2,1,0:T(8,128)S(1)}, u32[]{:S(2)}, u32[]{:S(2)}) collective-permute-start(f32[1,48,1536]{2,1,0:T(8,128)S(1)} %add.195.refs_2_), channel_id=1, source_target_pairs={{0,8},{4,12},{8,0},{12,4},{1,9},{5,13},{9,1},{13,5},{2,10},{6,14},... | collective-permute-start | bytes 884744 | tf_op jit(solution)/shard_map/ppermute | solution.py:189
  161.8 20.2 %copy-start.15 = (f32[48,1536]{1,0:T(8,128)S(1)}, f32[48,1536]{1,0:T(8,128)}, u32[]{:S(2)}) copy-start(f32[48,1536]{1,0:T(8,128)} %param.6) | copy-start | bytes 884740
  166.9 11.9 %collective-permute-start.20 = (f32[4,2,4,1536]{3,2,1,0:T(4,128)S(1)}, f32[4,2,4,1536]{3,2,1,0:T(4,128)S(1)}, u32[]{:S(2)}, u32[]{:S(2)}) collective-permute-start(f32[4,2,4,1536]{3,2,1,0:T(4,128)S(1)} %get-tuple-element.40), channel_id=1, source_target_pairs={{0,1},{1,2},{2,3},{4,5},{5,6},{6,7},{8,9},{9,10},{10,11},{12,13},{... | collective-permute-start | bytes 589832 | tf_op jit(solution)/shard_map/ppermute | solution.py:176
  168.2 12.5 %collective-permute-start.21 = (f32[4,2,4,1536]{3,2,1,0:T(4,128)S(1)}, f32[4,2,4,1536]{3,2,1,0:T(4,128)S(1)}, u32[]{:S(2)}, u32[]{:S(2)}) collective-permute-start(f32[4,2,4,1536]{3,2,1,0:T(4,128)S(1)} %get-tuple-element.39), channel_id=1, source_target_pairs={{1,0},{2,1},{3,2},{5,4},{6,5},{7,6},{9,8},{10,9},{11,10},{13,12},{... | collective-permute-start | bytes 589832 | tf_op jit(solution)/shard_map/ppermute | solution.py:176
  172.8 28.5 %collective-permute-start.14 = (f32[1,2,4,1536]{3,2,1,0:T(4,128)S(1)}, f32[1,2,4,1536]{3,2,1,0:T(4,128)S(1)}, u32[]{:S(2)}, u32[]{:S(2)}) collective-permute-start(f32[1,2,4,1536]{3,2,1,0:T(4,128)S(1)} %get-tuple-element.48), channel_id=1, source_target_pairs={{0,1},{1,2},{2,3},{4,5},{5,6},{6,7},{8,9},{9,10},{10,11},{12,13},{... | collective-permute-start | bytes 147464 | tf_op jit(solution)/shard_map/ppermute | solution.py:176
  174.1 27.2 %collective-permute-start.15 = (f32[1,2,4,1536]{3,2,1,0:T(4,128)S(1)}, f32[1,2,4,1536]{3,2,1,0:T(4,128)S(1)}, u32[]{:S(2)}, u32[]{:S(2)}) collective-permute-start(f32[1,2,4,1536]{3,2,1,0:T(4,128)S(1)} %get-tuple-element.47), channel_id=1, source_target_pairs={{1,0},{2,1},{3,2},{5,4},{6,5},{7,6},{9,8},{10,9},{11,10},{13,12},{... | collective-permute-start | bytes 147464 | tf_op jit(solution)/shard_map/ppermute | solution.py:176
  178.7 27.8 %collective-permute-start.10 = (f32[1,2,4,1536]{3,2,1,0:T(4,128)S(1)}, f32[1,2,4,1536]{3,2,1,0:T(4,128)S(1)}, u32[]{:S(2)}, u32[]{:S(2)}) collective-permute-start(f32[1,2,4,1536]{3,2,1,0:T(4,128)S(1)} %get-tuple-element.49), channel_id=1, source_target_pairs={{1,0},{2,1},{3,2},{5,4},{6,5},{7,6},{9,8},{10,9},{11,10},{13,12},{... | collective-permute-start | bytes 147464 | tf_op jit(solution)/shard_map/ppermute | solution.py:176
  180.7 25.8 %collective-permute-start.9 = (f32[1,2,4,1536]{3,2,1,0:T(4,128)S(1)}, f32[1,2,4,1536]{3,2,1,0:T(4,128)S(1)}, u32[]{:S(2)}, u32[]{:S(2)}) collective-permute-start(f32[1,2,4,1536]{3,2,1,0:T(4,128)S(1)} %get-tuple-element.50), channel_id=1, source_target_pairs={{0,1},{1,2},{2,3},{4,5},{5,6},{6,7},{8,9},{9,10},{10,11},{12,13},{... | collective-permute-start | bytes 147464 | tf_op jit(solution)/shard_map/ppermute | solution.py:176
  (16 other events, 86.8 us)
where the time goes:
time: 216 us; the launch traced here: 212 us
  waiting for transfers between devices  105 us (49%)
  Pallas kernels  51.9 us (24%)
  starting transfers between devices  38.9 us (18%)
  local copies, waits for them, and re-layouts  8.77 us (4%)
  other arithmetic  6.54 us (3%)
    ppermute x4, waiting for transfers between devices, compute(): parts.append(lax.ppermute(part, 'tm', pairs))  77.9 us
    ppermute x8, waiting for transfers between devices, halves_of_sum(): other = lax.ppermute(value, 'member', pairs)  27.2 us
    ppermute x10, starting transfers between devices, edges_from_neighbours(): return (lax.ppermute(bottom, 'state', up), lax.ppermute(top, 'state', down))  27.2 us
    pallas_call x2, Pallas kernels, mixed_levels(): pl.pallas_call(functools.partial(mix_kernel, chunks, lanes), grid=(rows /...  26.7 us
    pallas_call x4, Pallas kernels, filtered(): pl.pallas_call(functools.partial(filter_kernel, len(fields), halo, 1.0 /...  25.2 us
    ppermute x8, starting transfers between devices, halves_of_sum(): other = lax.ppermute(value, 'member', pairs)  6.59 us
    ppermute x4, starting transfers between devices, compute(): parts.append(lax.ppermute(part, 'tm', pairs))  5.09 us
  transfers between devices with their start and end apart: 22, of which 7 were waited for; matrix products, arithmetic and copies ran while one was open for 3% of the time, Pallas kernels for 16%

commit v1 on v0

--- a/solution.py
+++ b/solution.py
@@ -13,13 +13,8 @@
 
 
 def level_chunks(count):
-    sizes, left = [], count
-    while left > 0:
-        size = max(left // 2, 1)
-        sizes.append(size)
-        left -= size
-    starts = [sum(sizes[:i]) for i in range(len(sizes))]
-    return list(zip(starts, sizes))
+    first = count - count // 2
+    return [(0, first), (first, count - first)] if count > first else [(0, first)]
 
 
 def divisor(length, unit, most):
@@ -207,12 +202,21 @@
         chosen = lax.dynamic_slice_in_dim(scaled, first, own, 0)
         return (chosen[:, None, :, None] * eye[None, :, None, :]).reshape(own * SUB, levels * SUB)
 
+    share = 1.0 / ensemble
+
+    def member_sums(fields):
+        local = functools.reduce(jnp.add, [f[:, k] for f in fields for k in range(f.shape[1])])
+        return halves_of_sum(local)
+
     arrived = []
     for shift in range(1, groups):
         outgoing = mixed_levels(members, slot_grad, weights(shift), chunks)
         pairs = [(i, (i + shift) % groups) for i in range(groups)]
         parts = []
-        for part in outgoing:
+        for index, part in enumerate(outgoing):
+            if index:
+                total = member_sums([part])
+                part = part - ((total[0] + total[1]) * share)[:, None]
             parts.append(lax.ppermute(part, "tm", pairs))
         arrived.append(parts)
     mine = mixed_levels(members, slot_grad, weights(0), chunks)
@@ -221,25 +225,18 @@
     blank = jnp.zeros((SUB - halo, diffusivity.shape[1]), jnp.float32)
     rate = jnp.concatenate([blank, above, diffusivity, below, blank], axis=0)
 
-    staged, before = [], None
-    for index in range(len(chunks)):
-        received = [parts[index] for parts in arrived]
-        if before is not None:
-            received, before = lax.optimization_barrier((received, before))
-        fields = [mine[index]] + received
-        local = functools.reduce(jnp.add, [f[:, k] for f in fields for k in range(f.shape[1])])
-        before, other = halves_of_sum(local)
-        staged.append([fields, before, other])
+    early = [member_sums([part]) for part in mine[1:]]
+    first = [mine[0]] + [parts[0] for parts in arrived]
+    centres = [member_sums(first), *early]
 
     result = None
     for index, (start, size) in enumerate(chunks):
-        fields, *sums = staged[index]
-        if index + 1 < len(chunks):
-            sums, _ = lax.optimization_barrier((sums, staged[index + 1][1]))
+        fields = [mine[index]] + [parts[index] for parts in arrived]
+        sums = centres[index]
 
         def edge(at):
             value = functools.reduce(jnp.add, [f[:, :, at] for f in fields])
-            return value - (sums[0][:, at] + sums[1][:, at])[:, None] * (1.0 / ensemble)
+            return value - (sums[0][:, at] + sums[1][:, at])[:, None] * share
 
         halos = edges_from_neighbours(edge(slice(0, halo)), edge(slice(rows - halo, rows)))
         result = filtered(fields, sums, halos, rate, start, own, ensemble, result)

time: 216 us -> 179 us (0.83)
  the two profiles are of different devices: /device:TPU:24 before, /device:TPU:0 now
where the time goes in v1:
time: 179 us; the launch traced here: 178 us
  waiting for transfers between devices  79.4 us (44%)
  Pallas kernels  49.1 us (27%)
  starting transfers between devices  25.3 us (14%)
  local copies, waits for them, and re-layouts  14.6 us (8%)
  other arithmetic  9.42 us (5%)
    ppermute x6, waiting for transfers between devices, halves_of_sum(): other = lax.ppermute(value, 'member', pairs)  39.9 us
    ppermute x2, waiting for transfers between devices, compute(): parts.append(lax.ppermute(part, 'tm', pairs))  33.3 us
    pallas_call x2, Pallas kernels, mixed_levels(): pl.pallas_call(functools.partial(mix_kernel, chunks, lanes), grid=(rows /...  27.4 us
    pallas_call x2, Pallas kernels, filtered(): pl.pallas_call(functools.partial(filter_kernel, len(fields), halo, 1.0 /...  21.6 us
    ppermute x6, starting transfers between devices, edges_from_neighbours(): return (lax.ppermute(bottom, 'state', up), lax.ppermute(top, 'state', down))  15.6 us
    ppermute x6, waiting for transfers between devices, edges_from_neighbours(): return (lax.ppermute(bottom, 'state', up), lax.ppermute(top, 'state', down))  6.23 us
    ppermute x6, starting transfers between devices, halves_of_sum(): other = lax.ppermute(value, 'member', pairs)  4.89 us
    ppermute x2, starting transfers between devices, compute(): parts.append(lax.ppermute(part, 'tm', pairs))  4.78 us
  transfers between devices with their start and end apart: 14, of which 7 were waited for; matrix products, arithmetic and copies ran while one was open for 9% of the time, Pallas kernels for 14%

profile of v1, /device:TPU:0, one launch (start us, length us, event | category | flops | bytes accessed | tf_op | source)
XLA Modules:
  0.0 178.1 jit_solution(2125515625582472080)
XLA Ops:
  0.0 0.7 broadcast_multiply_fusion.2
  1.1 0.8 mul.79.w_ref
  1.9 13.7 %mix.3 = (f32[4,2,48,1536]{3,2,1,0:T(8,128)}, f32[4,2,48,1536]{3,2,1,0:T(8,128)}) custom-call(f32[64,128]{1,0:T(8,128)} %mul.79.w_ref, bf16[2,2,16,48,1536]{4,3,2,1,0:T(8,128)(2,1)} %members_ref.3, f32[2,16,48,1536]{3,2,1,0:T(8,128)} %grad_ref.3), custom_call_target="tpu_custom_call" | custom-call | flops 905969664 | bytes 18874368 | tf_op jit(solution)/shard_map/mix/pallas_call | solution.py:65
  15.6 3.4 %copy.22 = f32[4,2,48,1536]{3,2,0,1:T(8,128)} copy(f32[4,2,48,1536]{3,2,1,0:T(8,128)} %get-tuple-element.12) | data formatting | bytes 4718592 | tf_op jit(solution)/shard_map/mix/pallas_call | solution.py:65
  19.0 3.0 %collective-permute-start.9 = (f32[4,2,48,1536]{3,2,0,1:T(8,128)}, f32[4,2,48,1536]{3,2,0,1:T(8,128)}, u32[]{:S(2)}, u32[]{:S(2)}) collective-permute-start(f32[4,2,48,1536]{3,2,0,1:T(8,128)} %copy.22), channel_id=1, source_target_pairs={{0,16},{16,0},{1,17},{17,1},{2,18},{18,2},{3,19},{19,3},{4,20},{20... | collective-permute-start | bytes 7077896 | tf_op jit(solution)/shard_map/ppermute | solution.py:220
  22.2 0.8 mul.75.w_ref
  23.0 13.7 %mix.2 = (f32[4,2,48,1536]{3,2,1,0:T(8,128)}, f32[4,2,48,1536]{3,2,1,0:T(8,128)}) custom-call(f32[64,128]{1,0:T(8,128)} %mul.75.w_ref, bf16[2,2,16,48,1536]{4,3,2,1,0:T(8,128)(2,1)} %members_ref.3, f32[2,16,48,1536]{3,2,1,0:T(8,128)} %grad_ref.3), custom_call_target="tpu_custom_call" | custom-call | flops 905969664 | bytes 18874368 | tf_op jit(solution)/shard_map/mix/pallas_call | solution.py:65
  36.8 1.9 %fusion.1 = f32[4,48,1536]{2,1,0:T(8,128)S(1)} fusion(f32[4,2,48,1536]{3,2,1,0:T(8,128)} %get-tuple-element.9.refs_0_), kind=kLoop, calls=%fused_computation.5 | loop fusion | flops 294912 | bytes 3538944 | tf_op jit(solution)/shard_map/add | solution.py:208
  39.3 1.7 fusion.13
  41.0 1.6 collective-permute-start.1
  42.8 0.8 collective-permute-start.4
  43.6 29.9 %collective-permute-done.9 = f32[4,2,48,1536]{3,2,0,1:T(8,128)} collective-permute-done((f32[4,2,48,1536]{3,2,0,1:T(8,128)}, f32[4,2,48,1536]{3,2,0,1:T(8,128)}, u32[]{:S(2)}, u32[]{:S(2)}) %collective-permute-start.9) | collective-permute-done | bytes 2359328 | tf_op jit(solution)/shard_map/ppermute | solution.py:220
  73.5 2.1 %fusion = f32[4,48,1536]{2,1,0:T(8,128)S(1)} fusion(f32[4,2,48,1536]{3,2,0,1:T(8,128)} %collective-permute-done.9, f32[4,2,48,1536]{3,2,1,0:T(8,128)S(1)} %copy-done.3), kind=kLoop, calls=%fused_computation.1 | loop fusion | flops 884736 | bytes 5898240 | tf_op jit(solution)/shard_map/add | solution.py:208
  76.1 1.8 %collective-permute-start.2 = (f32[4,2,48,1536]{3,2,1,0:T(8,128)S(1)}, f32[4,2,48,1536]{3,2,1,0:T(8,128)S(1)}, u32[]{:S(2)}, u32[]{:S(2)}) collective-permute-start(f32[4,2,48,1536]{3,2,1,0:T(8,128)S(1)} %broadcast_subtract_fusion), channel_id=1, source_target_pairs={{0,16},{16,0},{1,17},{17,1},{2,18},{18,2},{3,19},{19,3},{4,20},{20... | collective-permute-start | bytes 7077896 | tf_op jit(solution)/shard_map/ppermute | solution.py:220
  78.7 1.8 %collective-permute-start.11 = (f32[4,48,1536]{2,1,0:T(8,128)S(1)}, f32[4,48,1536]{2,1,0:T(8,128)S(1)}, u32[]{:S(2)}, u32[]{:S(2)}) collective-permute-start(f32[4,48,1536]{2,1,0:T(8,128)S(1)} %add.89.refs_2_), channel_id=1, source_target_pairs={{0,8},{4,12},{8,0},{12,4},{1,9},{5,13},{9,1},{13,5},{2,10},{6,14},... | collective-permute-start | bytes 3538952 | tf_op jit(solution)/shard_map/ppermute | solution.py:184
  80.5 14.7 %collective-permute-done.4.refs_3_ = f32[4,48,1536]{2,1,0:T(8,128)S(1)} collective-permute-done((f32[4,48,1536]{2,1,0:T(8,128)S(1)}, f32[4,48,1536]{2,1,0:T(8,128)S(1)}, u32[]{:S(2)}, u32[]{:S(2)}) %collective-permute-start.4) | collective-permute-done | bytes 1179680 | tf_op jit(solution)/shard_map/ppermute | solution.py:184
  95.2 24.7 %collective-permute-done.11.refs_3_ = f32[4,48,1536]{2,1,0:T(8,128)S(1)} collective-permute-done((f32[4,48,1536]{2,1,0:T(8,128)S(1)}, f32[4,48,1536]{2,1,0:T(8,128)S(1)}, u32[]{:S(2)}, u32[]{:S(2)}) %collective-permute-start.11) | collective-permute-done | bytes 1179680 | tf_op jit(solution)/shard_map/ppermute | solution.py:184
  120.0 1.6 fusion.2
  121.7 3.5 %collective-permute-start.12 = (f32[4,2,4,1536]{3,2,0,1:T(4,128)S(1)}, f32[4,2,4,1536]{3,2,0,1:T(4,128)S(1)}, u32[]{:S(2)}, u32[]{:S(2)}) collective-permute-start(f32[4,2,4,1536]{3,2,0,1:T(4,128)S(1)} %get-tuple-element.14), channel_id=1, source_target_pairs={{0,1},{1,2},{2,3},{4,5},{5,6},{6,7},{8,9},{9,10},{10,11},{12,13},{... | collective-permute-start | bytes 589832 | tf_op jit(solution)/shard_map/ppermute | solution.py:171
  125.2 1.3 collective-permute-start.13
  126.5 3.3 %collective-permute-done.2.refs_1_ = f32[4,2,48,1536]{3,2,1,0:T(8,128)S(1)} collective-permute-done((f32[4,2,48,1536]{3,2,1,0:T(8,128)S(1)}, f32[4,2,48,1536]{3,2,1,0:T(8,128)S(1)}, u32[]{:S(2)}, u32[]{:S(2)}) %collective-permute-start.2) | collective-permute-done | bytes 2359328 | tf_op jit(solution)/shard_map/ppermute | solution.py:220
  130.0 1.3 copy-done.6
  131.3 3.7 %collective-permute-start.5 = (f32[4,2,4,1536]{3,2,1,0:T(4,128)S(1)}, f32[4,2,4,1536]{3,2,1,0:T(4,128)S(1)}, u32[]{:S(2)}, u32[]{:S(2)}) collective-permute-start(f32[4,2,4,1536]{3,2,1,0:T(4,128)S(1)} %get-tuple-element.16), channel_id=1, source_target_pairs={{0,1},{1,2},{2,3},{4,5},{5,6},{6,7},{8,9},{9,10},{10,11},{12,13},{... | collective-permute-start | bytes 589832 | tf_op jit(solution)/shard_map/ppermute | solution.py:171
  135.0 1.3 collective-permute-start.6
  136.4 4.5 %collective-permute-start.7 = (f32[4,1536]{1,0:T(4,128)S(1)}, f32[4,1536]{1,0:T(4,128)S(1)}, u32[]{:S(2)}, u32[]{:S(2)}) collective-permute-start(f32[4,1536]{1,0:T(4,128)S(1)} %get-tuple-element.22), channel_id=1, source_target_pairs={{0,1},{1,2},{2,3},{4,5},{5,6},{6,7},{8,9},{9,10},{10,11},{12,13},{... | collective-permute-start | bytes 73736 | tf_op jit(solution)/shard_map/ppermute | solution.py:171
  140.9 1.5 collective-permute-done.7
  142.4 1.3 collective-permute-start.8
  143.7 4.7 %collective-permute-done.8 = f32[4,1536]{1,0:T(4,128)S(1)} collective-permute-done((f32[4,1536]{1,0:T(4,128)S(1)}, f32[4,1536]{1,0:T(4,128)S(1)}, u32[]{:S(2)}, u32[]{:S(2)}) %collective-permute-start.8) | collective-permute-done | bytes 24608 | tf_op jit(solution)/shard_map/ppermute | solution.py:171
  148.4 2.1 %concatenate.3.refs_6_ = f32[64,1536]{1,0:T(8,128)} concatenate(f32[4,1536]{1,0:T(4,128)S(1)} %broadcast_in_dim.2, f32[4,1536]{1,0:T(4,128)S(1)} %collective-permute-done.7, f32[48,1536]{1,0:T(8,128)S(1)} %copy-done.9, f32[4,1536]{1,0:T(4,128)S(1)} %collective-permute-done.8, f32[4,1536]{1,0:T(4,128)S(1)} %broadcast_in_dim.2), dimensions={0} | concatenate | bytes 786432 | tf_op jit(solution)/shard_map/concatenate | solution.py:226
  150.5 3.2 %copy.27.refs_1_ = f32[4,2,48,1536]{3,2,1,0:T(8,128)} copy(f32[4,2,48,1536]{3,2,0,1:T(8,128)} %collective-permute-done.9) | data formatting | bytes 4718592 | tf_op jit(solution)/shard_map/ppermute | solution.py:220
  155.1 10.8 %filter.2.refs_7_ = f32[8,2,48,1536]{3,2,1,0:T(8,128)} custom-call(f32[4,2,48,1536]{3,2,1,0:T(8,128)} %get-tuple-element.11.refs_0_, f32[4,2,48,1536]{3,2,1,0:T(8,128)} %copy.27.refs_1_, f32[4,48,1536]{2,1,0:T(8,128)} %copy-done.4, f32[4,48,1536]{2,1,0:T(8,128)} %copy-done.8, f32[4,2,4,1536]{3,2,1,0:T(4,128)} %copy.28.refs_4_, ...), custom_call_target="tpu_custom_call" | custom-call | flops 94371840 | bytes 9437184 | tf_op jit(solution)/shard_map/filter/pallas_call | solution.py:147
  167.3 10.8 %filter.3 = f32[8,2,48,1536]{3,2,1,0:T(8,128)} custom-call(f32[4,2,48,1536]{3,2,1,0:T(8,128)} %get-tuple-element.9.refs_0_, f32[4,2,48,1536]{3,2,1,0:T(8,128)} %copy-done.6, f32[4,48,1536]{2,1,0:T(8,128)} %copy-done.5, f32[4,48,1536]{2,1,0:T(8,128)} %copy-done.7, f32[4,2,4,1536]{3,2,1,0:T(4,128)} %copy-done.10, ...), custom_call_target="tpu_custom_call", output_to_operand_aliasing={{}: (7, {})} | custom-call | flops 94371840 | bytes 9437184 | tf_op jit(solution)/shard_map/filter/pallas_call | solution.py:147
  (51 shorter events, 5.7 us)
Async XLA Ops:
  15.6 6.4 %copy-start.1 = (f32[4,2,48,1536]{3,2,1,0:T(8,128)S(1)}, f32[4,2,48,1536]{3,2,1,0:T(8,128)}, u32[]{:S(2)}) copy-start(f32[4,2,48,1536]{3,2,1,0:T(8,128)} %get-tuple-element.10) | copy-start | bytes 7077892
  19.0 54.5 %collective-permute-start.9 = (f32[4,2,48,1536]{3,2,0,1:T(8,128)}, f32[4,2,48,1536]{3,2,0,1:T(8,128)}, u32[]{:S(2)}, u32[]{:S(2)}) collective-permute-start(f32[4,2,48,1536]{3,2,0,1:T(8,128)} %copy.22), channel_id=1, source_target_pairs={{0,16},{16,0},{1,17},{17,1},{2,18},{18,2},{3,19},{19,3},{4,20},{20... | collective-permute-start | bytes 7077896 | tf_op jit(solution)/shard_map/ppermute | solution.py:220
  22.1 17.2 %collective-permute-start = (f32[4,48,1536]{2,1,0:T(8,128)S(1)}, f32[4,48,1536]{2,1,0:T(8,128)}, u32[]{:S(2)}, u32[]{:S(2)}) collective-permute-start(f32[4,48,1536]{2,1,0:T(8,128)S(1)} %add_bitcast_fusion), channel_id=1, source_target_pairs={{0,4},{4,0},{8,12},{12,8},{1,5},{5,1},{9,13},{13,9},{2,6},{6,2},{1... | collective-permute-start | bytes 3538952 | tf_op jit(solution)/shard_map/ppermute | solution.py:184
  36.8 2.5 %copy-start.2 = (f32[4,2,48,1536]{3,2,1,0:T(8,128)S(1)}, f32[4,2,48,1536]{3,2,1,0:T(8,128)}, u32[]{:S(2)}) copy-start(f32[4,2,48,1536]{3,2,1,0:T(8,128)} %get-tuple-element.10) | copy-start | bytes 7077892
  38.7 3.9 %copy-start = (f32[4,2,48,1536]{3,2,1,0:T(8,128)S(1)}, f32[4,2,48,1536]{3,2,1,0:T(8,128)}, u32[]{:S(2)}) copy-start(f32[4,2,48,1536]{3,2,1,0:T(8,128)} %get-tuple-element.9.refs_0_) | copy-start | bytes 7077892
  38.7 3.9 %collective-permute-start.3 = (f32[4,48,1536]{2,1,0:T(8,128)S(1)}, f32[4,48,1536]{2,1,0:T(8,128)S(1)}, u32[]{:S(2)}, u32[]{:S(2)}) collective-permute-start(f32[4,48,1536]{2,1,0:T(8,128)S(1)} %fusion.1), channel_id=1, source_target_pairs={{0,4},{4,0},{8,12},{12,8},{1,5},{5,1},{9,13},{13,9},{2,6},{6,2},{1... | collective-permute-start | bytes 3538952 | tf_op jit(solution)/shard_map/ppermute | solution.py:184
  41.0 34.7 %collective-permute-start.1 = (f32[4,48,1536]{2,1,0:T(8,128)S(1)}, f32[4,48,1536]{2,1,0:T(8,128)S(1)}, u32[]{:S(2)}, u32[]{:S(2)}) collective-permute-start(f32[4,48,1536]{2,1,0:T(8,128)S(1)} %fusion.13), channel_id=1, source_target_pairs={{0,8},{4,12},{8,0},{12,4},{1,9},{5,13},{9,1},{13,5},{2,10},{6,14},... | collective-permute-start | bytes 3538952 | tf_op jit(solution)/shard_map/ppermute | solution.py:184
  42.6 31.0 %copy-start.3 = (f32[4,2,48,1536]{3,2,1,0:T(8,128)S(1)}, f32[4,2,48,1536]{3,2,1,0:T(8,128)}, u32[]{:S(2)}) copy-start(f32[4,2,48,1536]{3,2,1,0:T(8,128)} %get-tuple-element.11.refs_0_) | copy-start | bytes 7077892
  42.8 52.3 %copy-start.5 = (f32[4,48,1536]{2,1,0:T(8,128)}, f32[4,48,1536]{2,1,0:T(8,128)S(1)}, u32[]{:S(2)}) copy-start(f32[4,48,1536]{2,1,0:T(8,128)S(1)} %fusion.12.refs_2_) | copy-start | bytes 3538948
  42.8 52.3 %collective-permute-start.4 = (f32[4,48,1536]{2,1,0:T(8,128)S(1)}, f32[4,48,1536]{2,1,0:T(8,128)S(1)}, u32[]{:S(2)}, u32[]{:S(2)}) collective-permute-start(f32[4,48,1536]{2,1,0:T(8,128)S(1)} %fusion.12.refs_2_), channel_id=1, source_target_pairs={{0,8},{4,12},{8,0},{12,4},{1,9},{5,13},{9,1},{13,5},{2,10},{6,14},... | collective-permute-start | bytes 3538952 | tf_op jit(solution)/shard_map/ppermute | solution.py:184
  75.6 2.9 %collective-permute-start.10 = (f32[4,48,1536]{2,1,0:T(8,128)S(1)}, f32[4,48,1536]{2,1,0:T(8,128)S(1)}, u32[]{:S(2)}, u32[]{:S(2)}) collective-permute-start(f32[4,48,1536]{2,1,0:T(8,128)S(1)} %fusion), channel_id=1, source_target_pairs={{0,4},{4,0},{8,12},{12,8},{1,5},{5,1},{9,13},{13,9},{2,6},{6,2},{1... | collective-permute-start | bytes 3538952 | tf_op jit(solution)/shard_map/ppermute | solution.py:184
  76.1 53.7 %collective-permute-start.2 = (f32[4,2,48,1536]{3,2,1,0:T(8,128)S(1)}, f32[4,2,48,1536]{3,2,1,0:T(8,128)S(1)}, u32[]{:S(2)}, u32[]{:S(2)}) collective-permute-start(f32[4,2,48,1536]{3,2,1,0:T(8,128)S(1)} %broadcast_subtract_fusion), channel_id=1, source_target_pairs={{0,16},{16,0},{1,17},{17,1},{2,18},{18,2},{3,19},{19,3},{4,20},{20... | collective-permute-start | bytes 7077896 | tf_op jit(solution)/shard_map/ppermute | solution.py:220
  78.6 43.1 %copy-start.4 = (f32[4,48,1536]{2,1,0:T(8,128)}, f32[4,48,1536]{2,1,0:T(8,128)S(1)}, u32[]{:S(2)}) copy-start(f32[4,48,1536]{2,1,0:T(8,128)S(1)} %add.89.refs_2_) | copy-start | bytes 3538948
  78.7 41.3 %collective-permute-start.11 = (f32[4,48,1536]{2,1,0:T(8,128)S(1)}, f32[4,48,1536]{2,1,0:T(8,128)S(1)}, u32[]{:S(2)}, u32[]{:S(2)}) collective-permute-start(f32[4,48,1536]{2,1,0:T(8,128)S(1)} %add.89.refs_2_), channel_id=1, source_target_pairs={{0,8},{4,12},{8,0},{12,4},{1,9},{5,13},{9,1},{13,5},{2,10},{6,14},... | collective-permute-start | bytes 3538952 | tf_op jit(solution)/shard_map/ppermute | solution.py:184
  95.2 26.5 %copy-start.7 = (f32[4,48,1536]{2,1,0:T(8,128)}, f32[4,48,1536]{2,1,0:T(8,128)S(1)}, u32[]{:S(2)}) copy-start(f32[4,48,1536]{2,1,0:T(8,128)S(1)} %collective-permute-done.4.refs_3_) | copy-start | bytes 3538948
  120.0 10.1 %copy-start.8 = (f32[4,48,1536]{2,1,0:T(8,128)}, f32[4,48,1536]{2,1,0:T(8,128)S(1)}, u32[]{:S(2)}) copy-start(f32[4,48,1536]{2,1,0:T(8,128)S(1)} %collective-permute-done.11.refs_3_) | copy-start | bytes 3538948
  120.0 16.3 %copy-start.9 = (f32[48,1536]{1,0:T(8,128)S(1)}, f32[48,1536]{1,0:T(8,128)}, u32[]{:S(2)}) copy-start(f32[48,1536]{1,0:T(8,128)} %param.6) | copy-start | bytes 884740
  121.7 32.0 %collective-permute-start.12 = (f32[4,2,4,1536]{3,2,0,1:T(4,128)S(1)}, f32[4,2,4,1536]{3,2,0,1:T(4,128)S(1)}, u32[]{:S(2)}, u32[]{:S(2)}) collective-permute-start(f32[4,2,4,1536]{3,2,0,1:T(4,128)S(1)} %get-tuple-element.14), channel_id=1, source_target_pairs={{0,1},{1,2},{2,3},{4,5},{5,6},{6,7},{8,9},{9,10},{10,11},{12,13},{... | collective-permute-start | bytes 589832 | tf_op jit(solution)/shard_map/ppermute | solution.py:171
  125.2 29.2 %collective-permute-start.13 = (f32[4,2,4,1536]{3,2,0,1:T(4,128)S(1)}, f32[4,2,4,1536]{3,2,0,1:T(4,128)S(1)}, u32[]{:S(2)}, u32[]{:S(2)}) collective-permute-start(f32[4,2,4,1536]{3,2,0,1:T(4,128)S(1)} %get-tuple-element.13), channel_id=1, source_target_pairs={{1,0},{2,1},{3,2},{5,4},{6,5},{7,6},{9,8},{10,9},{11,10},{13,12},{... | collective-permute-start | bytes 589832 | tf_op jit(solution)/shard_map/ppermute | solution.py:171
  129.9 1.4 copy-start.6
  131.3 34.6 %collective-permute-start.5 = (f32[4,2,4,1536]{3,2,1,0:T(4,128)S(1)}, f32[4,2,4,1536]{3,2,1,0:T(4,128)S(1)}, u32[]{:S(2)}, u32[]{:S(2)}) collective-permute-start(f32[4,2,4,1536]{3,2,1,0:T(4,128)S(1)} %get-tuple-element.16), channel_id=1, source_target_pairs={{0,1},{1,2},{2,3},{4,5},{5,6},{6,7},{8,9},{9,10},{10,11},{12,13},{... | collective-permute-start | bytes 589832 | tf_op jit(solution)/shard_map/ppermute | solution.py:171
  135.0 30.9 %collective-permute-start.6 = (f32[4,2,4,1536]{3,2,1,0:T(4,128)S(1)}, f32[4,2,4,1536]{3,2,1,0:T(4,128)S(1)}, u32[]{:S(2)}, u32[]{:S(2)}) collective-permute-start(f32[4,2,4,1536]{3,2,1,0:T(4,128)S(1)} %get-tuple-element.15), channel_id=1, source_target_pairs={{1,0},{2,1},{3,2},{5,4},{6,5},{7,6},{9,8},{10,9},{11,10},{13,12},{... | collective-permute-start | bytes 589832 | tf_op jit(solution)/shard_map/ppermute | solution.py:171
  136.4 6.1 %collective-permute-start.7 = (f32[4,1536]{1,0:T(4,128)S(1)}, f32[4,1536]{1,0:T(4,128)S(1)}, u32[]{:S(2)}, u32[]{:S(2)}) collective-permute-start(f32[4,1536]{1,0:T(4,128)S(1)} %get-tuple-element.22), channel_id=1, source_target_pairs={{0,1},{1,2},{2,3},{4,5},{5,6},{6,7},{8,9},{9,10},{10,11},{12,13},{... | collective-permute-start | bytes 73736 | tf_op jit(solution)/shard_map/ppermute | solution.py:171
  142.4 6.0 %collective-permute-start.8 = (f32[4,1536]{1,0:T(4,128)S(1)}, f32[4,1536]{1,0:T(4,128)S(1)}, u32[]{:S(2)}, u32[]{:S(2)}) collective-permute-start(f32[4,1536]{1,0:T(4,128)S(1)} %get-tuple-element.21), channel_id=1, source_target_pairs={{1,0},{2,1},{3,2},{5,4},{6,5},{7,6},{9,8},{10,9},{11,10},{13,12},{... | collective-permute-start | bytes 73736 | tf_op jit(solution)/shard_map/ppermute | solution.py:171
  165.9 0.7 copy-start.10
  166.6 0.7 copy-start.11

commit v2 on v1

--- a/solution.py
+++ b/solution.py
@@ -50,7 +50,7 @@
                 ) + jnp.dot(low, x_high, preferred_element_type=jnp.float32)
                 y = y.reshape(-1, SUB, lanes)
                 for out_ref, (start, size) in zip(out_refs, chunks):
-                    out_ref[:, k, first : first + SUB, at] = y[start : start + size]
+                    out_ref[k, :, first : first + SUB, at] = y[start : start + size]
         return carry
 
     lax.fori_loop(0, cols // lanes, piece, 0)
@@ -60,7 +60,7 @@
     slots, ensemble, levels, rows, cols = members.shape
     row_block, col_block = divisor(rows, SUB, 16), divisor(cols, 128, 512)
     lanes = divisor(col_block, 128, 256)
-    shapes = [(size, ensemble, rows, cols) for _, size in chunks]
+    shapes = [(ensemble, size, rows, cols) for _, size in chunks]
     own = weights.shape[0] // SUB
     return pl.pallas_call(
         functools.partial(mix_kernel, chunks, lanes),
@@ -73,7 +73,7 @@
             pl.BlockSpec((slots, levels, row_block, col_block), lambda i, j: (0, 0, i, j)),
         ],
         out_specs=[
-            pl.BlockSpec((size, ensemble, row_block, col_block), lambda i, j: (0, 0, i, j))
+            pl.BlockSpec((ensemble, size, row_block, col_block), lambda i, j: (0, 0, i, j))
             for _, size in chunks
         ],
         out_shape=[jax.ShapeDtypeStruct(shape, jnp.float32) for shape in shapes],
@@ -131,11 +131,11 @@
 
 
 def filtered(fields, sums, halos, rate, start, total, ensemble, previous):
-    size, members, rows, cols = fields[0].shape
+    members, size, rows, cols = fields[0].shape
     halo = halos[0].shape[2]
-    plane = pl.BlockSpec((1, 1, rows, cols), lambda i, k: (i, k, 0, 0))
+    plane = pl.BlockSpec((1, 1, rows, cols), lambda i, k: (k, i, 0, 0))
     shared = pl.BlockSpec((1, rows, cols), lambda i, k: (i, 0, 0))
-    edge = pl.BlockSpec((1, 1, halo, cols), lambda i, k: (i, k, 0, 0))
+    edge = pl.BlockSpec((1, 1, halo, cols), lambda i, k: (k, i, 0, 0))
     operands = [*fields, *sums, *halos, rate]
     in_specs = [plane] * len(fields) + [shared] * 2 + [edge] * 2
     in_specs.append(pl.BlockSpec(rate.shape, lambda i, k: (0, 0)))
@@ -205,7 +205,7 @@
     share = 1.0 / ensemble
 
     def member_sums(fields):
-        local = functools.reduce(jnp.add, [f[:, k] for f in fields for k in range(f.shape[1])])
+        local = functools.reduce(jnp.add, [f[k] for f in fields for k in range(f.shape[0])])
         return halves_of_sum(local)
 
     arrived = []
@@ -216,7 +216,7 @@
         for index, part in enumerate(outgoing):
             if index:
                 total = member_sums([part])
-                part = part - ((total[0] + total[1]) * share)[:, None]
+                part = part - ((total[0] + total[1]) * share)[None]
             parts.append(lax.ppermute(part, "tm", pairs))
         arrived.append(parts)
     mine = mixed_levels(members, slot_grad, weights(0), chunks)
@@ -236,7 +236,7 @@
 
         def edge(at):
             value = functools.reduce(jnp.add, [f[:, :, at] for f in fields])
-            return value - (sums[0][:, at] + sums[1][:, at])[:, None] * share
+            return value - (sums[0][:, at] + sums[1][:, at])[None] * share
 
         halos = edges_from_neighbours(edge(slice(0, halo)), edge(slice(rows - halo, rows)))
         result = filtered(fields, sums, halos, rate, start, own, ensemble, result)

time: 179 us -> 172 us (0.961)
  local copies, waits for them, and re-layouts: 14.6 us -> 7.93 us
    ppermute x3 -> x0, local copies, waits for them, and re-layouts: 4.58 us -> none  [the longest x1 3.2 us: compute(): parts.append(lax.ppermute(part, 'tm', pairs))]
    pallas_call x1 -> x0, local copies, waits for them, and re-layouts: 3.4 us -> none  [mixed_levels(): pl.pallas_call(functools.partial(mix_kernel, chunks, lanes), grid=(rows /...]
    unnamed x24 -> x26, local copies, waits for them, and re-layouts: 2.67 us -> 3.99 us
  transfers between devices with their start and end apart: 14 -> 14, of which waited for: 7 -> 8; matrix products, arithmetic and copies ran while one was open for 9% -> 7% of each run, Pallas kernels for 14% -> 14%
where the time goes in v2:
time: 172 us; the launch traced here: 171 us
  waiting for transfers between devices  78.4 us (46%)
  Pallas kernels  49.1 us (29%)
  starting transfers between devices  26.1 us (15%)
  other arithmetic  9.62 us (6%)
  local copies, waits for them, and re-layouts  7.93 us (5%)
    ppermute x6, waiting for transfers between devices, halves_of_sum(): other = lax.ppermute(value, 'member', pairs)  40.7 us
    ppermute x2, waiting for transfers between devices, compute(): parts.append(lax.ppermute(part, 'tm', pairs))  31.6 us
    pallas_call x2, Pallas kernels, mixed_levels(): pl.pallas_call(functools.partial(mix_kernel, chunks, lanes), grid=(rows /...  27.4 us
    pallas_call x2, Pallas kernels, filtered(): pl.pallas_call(functools.partial(filter_kernel, len(fields), halo, 1.0 /...  21.6 us
    ppermute x6, starting transfers between devices, edges_from_neighbours(): return (lax.ppermute(bottom, 'state', up), lax.ppermute(top, 'state', down))  15.6 us
    ppermute x6, waiting for transfers between devices, edges_from_neighbours(): return (lax.ppermute(bottom, 'state', up), lax.ppermute(top, 'state', down))  6.23 us
    add x3, other arithmetic, member_sums(): functools.reduce(jnp.add, [f[k] for f in fields for k in range(f.shape[0])])  5.72 us
    ppermute x6, starting transfers between devices, halves_of_sum(): other = lax.ppermute(value, 'member', pairs)  5.7 us
  transfers between devices with their start and end apart: 14, of which 8 were waited for; matrix products, arithmetic and copies ran while one was open for 7% of the time, Pallas kernels for 14%

profile of v2, /device:TPU:0, one launch (start us, length us, event | category | flops | bytes accessed | tf_op | source)
XLA Modules:
  0.0 171.4 jit_solution(10270098637354038007)
XLA Ops:
  0.0 0.7 broadcast_multiply_fusion.2
  1.1 0.8 mul.79.w_ref
  1.9 13.7 %mix.3 = (f32[2,4,48,1536]{3,2,1,0:T(8,128)}, f32[2,4,48,1536]{3,2,1,0:T(8,128)}) custom-call(f32[64,128]{1,0:T(8,128)} %mul.79.w_ref, bf16[2,2,16,48,1536]{4,3,2,1,0:T(8,128)(2,1)} %members_ref.3, f32[2,16,48,1536]{3,2,1,0:T(8,128)} %grad_ref.3), custom_call_target="tpu_custom_call" | custom-call | flops 905969664 | bytes 18874368 | tf_op jit(solution)/shard_map/mix/pallas_call | solution.py:65
  15.6 3.0 %collective-permute-start.9 = (f32[2,4,48,1536]{3,2,1,0:T(8,128)}, f32[2,4,48,1536]{3,2,1,0:T(8,128)}, u32[]{:S(2)}, u32[]{:S(2)}) collective-permute-start(f32[2,4,48,1536]{3,2,1,0:T(8,128)} %get-tuple-element.12), channel_id=1, source_target_pairs={{0,16},{16,0},{1,17},{17,1},{2,18},{18,2},{3,19},{19,3},{4,20},{20... | collective-permute-start | bytes 7077896 | tf_op jit(solution)/shard_map/ppermute | solution.py:220
  18.6 1.8 %add_bitcast_fusion.1 = f32[4,48,1536]{2,1,0:T(8,128)S(1)} fusion(f32[2,4,48,1536]{3,2,1,0:T(8,128)} %get-tuple-element.10), kind=kLoop, calls=%fused_computation.6 | loop fusion | flops 294912 | bytes 3538944 | tf_op jit(solution)/shard_map/add | solution.py:208
  20.4 0.8 mul.75.w_ref
  21.3 13.7 %mix.2 = (f32[2,4,48,1536]{3,2,1,0:T(8,128)}, f32[2,4,48,1536]{3,2,1,0:T(8,128)}) custom-call(f32[64,128]{1,0:T(8,128)} %mul.75.w_ref, bf16[2,2,16,48,1536]{4,3,2,1,0:T(8,128)(2,1)} %members_ref.3, f32[2,16,48,1536]{3,2,1,0:T(8,128)} %grad_ref.3), custom_call_target="tpu_custom_call" | custom-call | flops 905969664 | bytes 18874368 | tf_op jit(solution)/shard_map/mix/pallas_call | solution.py:65
  35.0 1.9 %add_bitcast_fusion = f32[4,48,1536]{2,1,0:T(8,128)S(1)} fusion(f32[2,4,48,1536]{3,2,1,0:T(8,128)} %get-tuple-element.9.refs_0_), kind=kLoop, calls=%fused_computation.3 | loop fusion | flops 294912 | bytes 3538944 | tf_op jit(solution)/shard_map/add | solution.py:208
  37.8 1.6 collective-permute-start.1
  40.2 1.6 collective-permute-start.4
  41.8 28.3 %collective-permute-done.9.refs_1_ = f32[2,4,48,1536]{3,2,1,0:T(8,128)} collective-permute-done((f32[2,4,48,1536]{3,2,1,0:T(8,128)}, f32[2,4,48,1536]{3,2,1,0:T(8,128)}, u32[]{:S(2)}, u32[]{:S(2)}) %collective-permute-start.9) | collective-permute-done | bytes 2359328 | tf_op jit(solution)/shard_map/ppermute | solution.py:220
  70.1 2.1 %fusion = f32[4,48,1536]{2,1,0:T(8,128)S(1)} fusion(f32[2,4,48,1536]{3,2,1,0:T(8,128)} %collective-permute-done.9.refs_1_, f32[2,4,48,1536]{3,2,1,0:T(8,128)S(1)} %copy-done.2), kind=kLoop, calls=%fused_computation.1 | loop fusion | flops 884736 | bytes 5898240 | tf_op jit(solution)/shard_map/add | solution.py:208
  72.7 1.8 %collective-permute-start.2 = (f32[2,4,48,1536]{3,2,1,0:T(8,128)S(1)}, f32[2,4,48,1536]{3,2,1,0:T(8,128)S(1)}, u32[]{:S(2)}, u32[]{:S(2)}) collective-permute-start(f32[2,4,48,1536]{3,2,1,0:T(8,128)S(1)} %broadcast_subtract_fusion), channel_id=1, source_target_pairs={{0,16},{16,0},{1,17},{17,1},{2,18},{18,2},{3,19},{19,3},{4,20},{20... | collective-permute-start | bytes 7077896 | tf_op jit(solution)/shard_map/ppermute | solution.py:220
  75.3 1.8 %collective-permute-start.11 = (f32[4,48,1536]{2,1,0:T(8,128)S(1)}, f32[4,48,1536]{2,1,0:T(8,128)S(1)}, u32[]{:S(2)}, u32[]{:S(2)}) collective-permute-start(f32[4,48,1536]{2,1,0:T(8,128)S(1)} %add.89.refs_2_), channel_id=1, source_target_pairs={{0,8},{4,12},{8,0},{12,4},{1,9},{5,13},{9,1},{13,5},{2,10},{6,14},... | collective-permute-start | bytes 3538952 | tf_op jit(solution)/shard_map/ppermute | solution.py:184
  77.1 14.9 %collective-permute-done.4.refs_3_ = f32[4,48,1536]{2,1,0:T(8,128)S(1)} collective-permute-done((f32[4,48,1536]{2,1,0:T(8,128)S(1)}, f32[4,48,1536]{2,1,0:T(8,128)S(1)}, u32[]{:S(2)}, u32[]{:S(2)}) %collective-permute-start.4) | collective-permute-done | bytes 1179680 | tf_op jit(solution)/shard_map/ppermute | solution.py:184
  92.0 24.6 %collective-permute-done.11.refs_3_ = f32[4,48,1536]{2,1,0:T(8,128)S(1)} collective-permute-done((f32[4,48,1536]{2,1,0:T(8,128)S(1)}, f32[4,48,1536]{2,1,0:T(8,128)S(1)}, u32[]{:S(2)}, u32[]{:S(2)}) %collective-permute-start.11) | collective-permute-done | bytes 1179680 | tf_op jit(solution)/shard_map/ppermute | solution.py:184
  116.7 1.6 fusion.1
  118.4 3.5 %collective-permute-start.12 = (f32[2,4,4,1536]{3,2,1,0:T(4,128)S(1)}, f32[2,4,4,1536]{3,2,1,0:T(4,128)S(1)}, u32[]{:S(2)}, u32[]{:S(2)}) collective-permute-start(f32[2,4,4,1536]{3,2,1,0:T(4,128)S(1)} %get-tuple-element.14), channel_id=1, source_target_pairs={{0,1},{1,2},{2,3},{4,5},{5,6},{6,7},{8,9},{9,10},{10,11},{12,13},{... | collective-permute-start | bytes 589832 | tf_op jit(solution)/shard_map/ppermute | solution.py:171
  121.9 1.3 collective-permute-start.13
  123.2 3.2 %collective-permute-done.2.refs_1_ = f32[2,4,48,1536]{3,2,1,0:T(8,128)S(1)} collective-permute-done((f32[2,4,48,1536]{3,2,1,0:T(8,128)S(1)}, f32[2,4,48,1536]{3,2,1,0:T(8,128)S(1)}, u32[]{:S(2)}, u32[]{:S(2)}) %collective-permute-start.2) | collective-permute-done | bytes 2359328 | tf_op jit(solution)/shard_map/ppermute | solution.py:220
  126.6 1.3 copy-done.5
  127.9 3.7 %collective-permute-start.5 = (f32[2,4,4,1536]{3,2,1,0:T(4,128)S(1)}, f32[2,4,4,1536]{3,2,1,0:T(4,128)S(1)}, u32[]{:S(2)}, u32[]{:S(2)}) collective-permute-start(f32[2,4,4,1536]{3,2,1,0:T(4,128)S(1)} %get-tuple-element.16), channel_id=1, source_target_pairs={{0,1},{1,2},{2,3},{4,5},{5,6},{6,7},{8,9},{9,10},{10,11},{12,13},{... | collective-permute-start | bytes 589832 | tf_op jit(solution)/shard_map/ppermute | solution.py:171
  131.6 1.3 collective-permute-start.6
  132.9 4.5 %collective-permute-start.7 = (f32[4,1536]{1,0:T(4,128)S(1)}, f32[4,1536]{1,0:T(4,128)S(1)}, u32[]{:S(2)}, u32[]{:S(2)}) collective-permute-start(f32[4,1536]{1,0:T(4,128)S(1)} %get-tuple-element.22), channel_id=1, source_target_pairs={{0,1},{1,2},{2,3},{4,5},{5,6},{6,7},{8,9},{9,10},{10,11},{12,13},{... | collective-permute-start | bytes 73736 | tf_op jit(solution)/shard_map/ppermute | solution.py:171
  137.5 1.5 collective-permute-done.7
  139.0 1.3 collective-permute-start.8
  140.3 4.7 %collective-permute-done.8 = f32[4,1536]{1,0:T(4,128)S(1)} collective-permute-done((f32[4,1536]{1,0:T(4,128)S(1)}, f32[4,1536]{1,0:T(4,128)S(1)}, u32[]{:S(2)}, u32[]{:S(2)}) %collective-permute-start.8) | collective-permute-done | bytes 24608 | tf_op jit(solution)/shard_map/ppermute | solution.py:171
  145.0 2.1 %concatenate.3.refs_6_ = f32[64,1536]{1,0:T(8,128)} concatenate(f32[4,1536]{1,0:T(4,128)S(1)} %broadcast_in_dim.2, f32[4,1536]{1,0:T(4,128)S(1)} %collective-permute-done.7, f32[48,1536]{1,0:T(8,128)S(1)} %copy-done.8, f32[4,1536]{1,0:T(4,128)S(1)} %collective-permute-done.8, f32[4,1536]{1,0:T(4,128)S(1)} %broadcast_in_dim.2), dimensions={0} | concatenate | bytes 786432 | tf_op jit(solution)/shard_map/concatenate | solution.py:226
  148.4 10.8 %filter.2.refs_7_ = f32[8,2,48,1536]{3,2,1,0:T(8,128)} custom-call(f32[2,4,48,1536]{3,2,1,0:T(8,128)} %get-tuple-element.11.refs_0_, f32[2,4,48,1536]{3,2,1,0:T(8,128)} %collective-permute-done.9.refs_1_, f32[4,48,1536]{2,1,0:T(8,128)} %copy-done.3, f32[4,48,1536]{2,1,0:T(8,128)} %copy-done.7, f32[2,4,4,1536]{3,2,1,0:T(4,128)} %copy-done.11, ...), custom_call_target="tpu_custom_call" | custom-call | flops 94371840 | bytes 9437184 | tf_op jit(solution)/shard_map/filter/pallas_call | solution.py:147
  159.2 0.7 copy-done.9
  159.9 0.7 copy-done.10
  160.6 10.8 %filter.3 = f32[8,2,48,1536]{3,2,1,0:T(8,128)} custom-call(f32[2,4,48,1536]{3,2,1,0:T(8,128)} %get-tuple-element.9.refs_0_, f32[2,4,48,1536]{3,2,1,0:T(8,128)} %copy-done.5, f32[4,48,1536]{2,1,0:T(8,128)} %copy-done.4, f32[4,48,1536]{2,1,0:T(8,128)} %copy-done.6, f32[2,4,4,1536]{3,2,1,0:T(4,128)} %copy-done.9, ...), custom_call_target="tpu_custom_call", output_to_operand_aliasing={{}: (7, {})} | custom-call | flops 94371840 | bytes 9437184 | tf_op jit(solution)/shard_map/filter/pallas_call | solution.py:147
  (49 shorter events, 5.0 us)
Async XLA Ops:
  15.6 54.5 %collective-permute-start.9 = (f32[2,4,48,1536]{3,2,1,0:T(8,128)}, f32[2,4,48,1536]{3,2,1,0:T(8,128)}, u32[]{:S(2)}, u32[]{:S(2)}) collective-permute-start(f32[2,4,48,1536]{3,2,1,0:T(8,128)} %get-tuple-element.12), channel_id=1, source_target_pairs={{0,16},{16,0},{1,17},{17,1},{2,18},{18,2},{3,19},{19,3},{4,20},{20... | collective-permute-start | bytes 7077896 | tf_op jit(solution)/shard_map/ppermute | solution.py:220
  20.3 17.1 %collective-permute-start = (f32[4,48,1536]{2,1,0:T(8,128)S(1)}, f32[4,48,1536]{2,1,0:T(8,128)S(1)}, u32[]{:S(2)}, u32[]{:S(2)}) collective-permute-start(f32[4,48,1536]{2,1,0:T(8,128)S(1)} %add_bitcast_fusion.1), channel_id=1, source_target_pairs={{0,4},{4,0},{8,12},{12,8},{1,5},{5,1},{9,13},{13,9},{2,6},{6,2},{1... | collective-permute-start | bytes 3538952 | tf_op jit(solution)/shard_map/ppermute | solution.py:184
  35.0 2.5 %copy-start.1 = (f32[2,4,48,1536]{3,2,1,0:T(8,128)S(1)}, f32[2,4,48,1536]{3,2,1,0:T(8,128)}, u32[]{:S(2)}) copy-start(f32[2,4,48,1536]{3,2,1,0:T(8,128)} %get-tuple-element.10) | copy-start | bytes 7077892
  36.9 3.0 %collective-permute-start.3 = (f32[4,48,1536]{2,1,0:T(8,128)S(1)}, f32[4,48,1536]{2,1,0:T(8,128)S(1)}, u32[]{:S(2)}, u32[]{:S(2)}) collective-permute-start(f32[4,48,1536]{2,1,0:T(8,128)S(1)} %add_bitcast_fusion), channel_id=1, source_target_pairs={{0,4},{4,0},{8,12},{12,8},{1,5},{5,1},{9,13},{13,9},{2,6},{6,2},{1... | collective-permute-start | bytes 3538952 | tf_op jit(solution)/shard_map/ppermute | solution.py:184
  37.5 2.5 %copy-start = (f32[2,4,48,1536]{3,2,1,0:T(8,128)S(1)}, f32[2,4,48,1536]{3,2,1,0:T(8,128)}, u32[]{:S(2)}) copy-start(f32[2,4,48,1536]{3,2,1,0:T(8,128)} %get-tuple-element.9.refs_0_) | copy-start | bytes 7077892
  37.8 34.5 %collective-permute-start.1 = (f32[4,48,1536]{2,1,0:T(8,128)S(1)}, f32[4,48,1536]{2,1,0:T(8,128)S(1)}, u32[]{:S(2)}, u32[]{:S(2)}) collective-permute-start(f32[4,48,1536]{2,1,0:T(8,128)S(1)} %fusion.12), channel_id=1, source_target_pairs={{0,8},{4,12},{8,0},{12,4},{1,9},{5,13},{9,1},{13,5},{2,10},{6,14},... | collective-permute-start | bytes 3538952 | tf_op jit(solution)/shard_map/ppermute | solution.py:184
  39.9 30.2 %copy-start.2 = (f32[2,4,48,1536]{3,2,1,0:T(8,128)S(1)}, f32[2,4,48,1536]{3,2,1,0:T(8,128)}, u32[]{:S(2)}) copy-start(f32[2,4,48,1536]{3,2,1,0:T(8,128)} %get-tuple-element.11.refs_0_) | copy-start | bytes 7077892
  40.2 51.8 %copy-start.4 = (f32[4,48,1536]{2,1,0:T(8,128)}, f32[4,48,1536]{2,1,0:T(8,128)S(1)}, u32[]{:S(2)}) copy-start(f32[4,48,1536]{2,1,0:T(8,128)S(1)} %fusion.11.refs_2_) | copy-start | bytes 3538948
  40.2 51.7 %collective-permute-start.4 = (f32[4,48,1536]{2,1,0:T(8,128)S(1)}, f32[4,48,1536]{2,1,0:T(8,128)S(1)}, u32[]{:S(2)}, u32[]{:S(2)}) collective-permute-start(f32[4,48,1536]{2,1,0:T(8,128)S(1)} %fusion.11.refs_2_), channel_id=1, source_target_pairs={{0,8},{4,12},{8,0},{12,4},{1,9},{5,13},{9,1},{13,5},{2,10},{6,14},... | collective-permute-start | bytes 3538952 | tf_op jit(solution)/shard_map/ppermute | solution.py:184
  72.2 2.9 %collective-permute-start.10 = (f32[4,48,1536]{2,1,0:T(8,128)S(1)}, f32[4,48,1536]{2,1,0:T(8,128)S(1)}, u32[]{:S(2)}, u32[]{:S(2)}) collective-permute-start(f32[4,48,1536]{2,1,0:T(8,128)S(1)} %fusion), channel_id=1, source_target_pairs={{0,4},{4,0},{8,12},{12,8},{1,5},{5,1},{9,13},{13,9},{2,6},{6,2},{1... | collective-permute-start | bytes 3538952 | tf_op jit(solution)/shard_map/ppermute | solution.py:184
  72.7 53.7 %collective-permute-start.2 = (f32[2,4,48,1536]{3,2,1,0:T(8,128)S(1)}, f32[2,4,48,1536]{3,2,1,0:T(8,128)S(1)}, u32[]{:S(2)}, u32[]{:S(2)}) collective-permute-start(f32[2,4,48,1536]{3,2,1,0:T(8,128)S(1)} %broadcast_subtract_fusion), channel_id=1, source_target_pairs={{0,16},{16,0},{1,17},{17,1},{2,18},{18,2},{3,19},{19,3},{4,20},{20... | collective-permute-start | bytes 7077896 | tf_op jit(solution)/shard_map/ppermute | solution.py:220
  75.3 43.1 %copy-start.3 = (f32[4,48,1536]{2,1,0:T(8,128)}, f32[4,48,1536]{2,1,0:T(8,128)S(1)}, u32[]{:S(2)}) copy-start(f32[4,48,1536]{2,1,0:T(8,128)S(1)} %add.89.refs_2_) | copy-start | bytes 3538948
  75.3 41.4 %collective-permute-start.11 = (f32[4,48,1536]{2,1,0:T(8,128)S(1)}, f32[4,48,1536]{2,1,0:T(8,128)S(1)}, u32[]{:S(2)}, u32[]{:S(2)}) collective-permute-start(f32[4,48,1536]{2,1,0:T(8,128)S(1)} %add.89.refs_2_), channel_id=1, source_target_pairs={{0,8},{4,12},{8,0},{12,4},{1,9},{5,13},{9,1},{13,5},{2,10},{6,14},... | collective-permute-start | bytes 3538952 | tf_op jit(solution)/shard_map/ppermute | solution.py:184
  92.0 26.4 %copy-start.6 = (f32[4,48,1536]{2,1,0:T(8,128)}, f32[4,48,1536]{2,1,0:T(8,128)S(1)}, u32[]{:S(2)}) copy-start(f32[4,48,1536]{2,1,0:T(8,128)S(1)} %collective-permute-done.4.refs_3_) | copy-start | bytes 3538948
  116.7 10.0 %copy-start.7 = (f32[4,48,1536]{2,1,0:T(8,128)}, f32[4,48,1536]{2,1,0:T(8,128)S(1)}, u32[]{:S(2)}) copy-start(f32[4,48,1536]{2,1,0:T(8,128)S(1)} %collective-permute-done.11.refs_3_) | copy-start | bytes 3538948
  116.7 16.2 %copy-start.8 = (f32[48,1536]{1,0:T(8,128)S(1)}, f32[48,1536]{1,0:T(8,128)}, u32[]{:S(2)}) copy-start(f32[48,1536]{1,0:T(8,128)} %param.6) | copy-start | bytes 884740
  118.4 28.6 %collective-permute-start.12 = (f32[2,4,4,1536]{3,2,1,0:T(4,128)S(1)}, f32[2,4,4,1536]{3,2,1,0:T(4,128)S(1)}, u32[]{:S(2)}, u32[]{:S(2)}) collective-permute-start(f32[2,4,4,1536]{3,2,1,0:T(4,128)S(1)} %get-tuple-element.14), channel_id=1, source_target_pairs={{0,1},{1,2},{2,3},{4,5},{5,6},{6,7},{8,9},{9,10},{10,11},{12,13},{... | collective-permute-start | bytes 589832 | tf_op jit(solution)/shard_map/ppermute | solution.py:171
  121.9 25.1 %collective-permute-start.13 = (f32[2,4,4,1536]{3,2,1,0:T(4,128)S(1)}, f32[2,4,4,1536]{3,2,1,0:T(4,128)S(1)}, u32[]{:S(2)}, u32[]{:S(2)}) collective-permute-start(f32[2,4,4,1536]{3,2,1,0:T(4,128)S(1)} %get-tuple-element.13), channel_id=1, source_target_pairs={{1,0},{2,1},{3,2},{5,4},{6,5},{7,6},{9,8},{10,9},{11,10},{13,12},{... | collective-permute-start | bytes 589832 | tf_op jit(solution)/shard_map/ppermute | solution.py:171
  126.4 1.4 copy-start.5
  127.9 31.3 %collective-permute-start.5 = (f32[2,4,4,1536]{3,2,1,0:T(4,128)S(1)}, f32[2,4,4,1536]{3,2,1,0:T(4,128)S(1)}, u32[]{:S(2)}, u32[]{:S(2)}) collective-permute-start(f32[2,4,4,1536]{3,2,1,0:T(4,128)S(1)} %get-tuple-element.16), channel_id=1, source_target_pairs={{0,1},{1,2},{2,3},{4,5},{5,6},{6,7},{8,9},{9,10},{10,11},{12,13},{... | collective-permute-start | bytes 589832 | tf_op jit(solution)/shard_map/ppermute | solution.py:171
  131.6 27.6 %collective-permute-start.6 = (f32[2,4,4,1536]{3,2,1,0:T(4,128)S(1)}, f32[2,4,4,1536]{3,2,1,0:T(4,128)S(1)}, u32[]{:S(2)}, u32[]{:S(2)}) collective-permute-start(f32[2,4,4,1536]{3,2,1,0:T(4,128)S(1)} %get-tuple-element.15), channel_id=1, source_target_pairs={{1,0},{2,1},{3,2},{5,4},{6,5},{7,6},{9,8},{10,9},{11,10},{13,12},{... | collective-permute-start | bytes 589832 | tf_op jit(solution)/shard_map/ppermute | solution.py:171
  132.9 6.1 %collective-permute-start.7 = (f32[4,1536]{1,0:T(4,128)S(1)}, f32[4,1536]{1,0:T(4,128)S(1)}, u32[]{:S(2)}, u32[]{:S(2)}) collective-permute-start(f32[4,1536]{1,0:T(4,128)S(1)} %get-tuple-element.22), channel_id=1, source_target_pairs={{0,1},{1,2},{2,3},{4,5},{5,6},{6,7},{8,9},{9,10},{10,11},{12,13},{... | collective-permute-start | bytes 73736 | tf_op jit(solution)/shard_map/ppermute | solution.py:171
  139.0 6.0 %collective-permute-start.8 = (f32[4,1536]{1,0:T(4,128)S(1)}, f32[4,1536]{1,0:T(4,128)S(1)}, u32[]{:S(2)}, u32[]{:S(2)}) collective-permute-start(f32[4,1536]{1,0:T(4,128)S(1)} %get-tuple-element.21), channel_id=1, source_target_pairs={{1,0},{2,1},{3,2},{5,4},{6,5},{7,6},{9,8},{10,9},{11,10},{13,12},{... | collective-permute-start | bytes 73736 | tf_op jit(solution)/shard_map/ppermute | solution.py:171
  147.1 0.7 copy-start.11
  147.7 0.7 copy-start.12
  159.2 0.7 copy-start.9
  159.9 0.7 copy-start.10
